TPU v7x, 128 devices: a whole 4x4x4 slice. The times are simulated.
128 devices in a mesh: tp: 8 (over y, x_hi), dp: 16 (over z, x_lo, core).
Axes of the slice: x: 4 (x_hi: 2, x_lo: 2; x = x_hi * 2 + x_lo), y: 4, z: 4, core: 2. Of those that a mesh axis runs over, the one named last changes fastest.
Arguments:
- activations: bfloat16 [2, 16384, 8192], P(None, 'dp', 'tp'), may hold values from -72 to 72
- out_grads: bfloat16 [2, 16384, 2048], P(None, 'dp'), may hold values from -2 to 2
- master: float32 [8192, 2, 2048], P(('tp', 'dp')), may hold values from -1.2 to 1.2
- first_moment: float32 [8192, 2, 2048], P(('tp', 'dp')), may hold values from -1.8 to 1.8
- second_moment: float32 [8192, 2, 2048], P(('tp', 'dp')), may hold values from 0.01 to 1
Outputs:
- new_master: float32 [8192, 2, 2048], P(('tp', 'dp'))
- new_first: float32 [8192, 2, 2048], P(('tp', 'dp'))
- new_second: float32 [8192, 2, 2048], P(('tp', 'dp'))
- weights: bfloat16 [8192, 2, 2048], P('tp')
All inputs are finite; a program needn't handle non-finite values.
Results may differ from a plain program's by a relative error of at most 0.0004.
Values may be sent and summed in bfloat16 or wider, within the bound.
A program may use at most 128 MiB of HBM per device.

v0:
```python
import functools
import math

import jax
import jax.numpy as jnp
from jax import lax
from jax.sharding import Mesh
from jax.sharding import PartitionSpec as P

DP = ("dp_0", "dp_1", "dp_2")
TP_DP = ("tp_0", "tp_1", "dp_0", "dp_1", "dp_2")
TP = ("tp_0", "tp_1")


beta_first = 0.9
beta_second = 0.95
first_fix = 1.0 - 0.9**10
second_fix = 1.0 - 0.95**10
learn_rate = 0.01
decay_rate = 0.1
epsilon = 1e-08
limit_scale = 2.0


def cut_along(array, dim, peers):
    dims = array.shape
    blocks = array.reshape(*dims[:dim], peers, dims[dim] // peers, *dims[dim + 1 :])
    return jnp.moveaxis(blocks, dim, 0)


def scatter_pairs(array, chips, core, dim):
    sizes = (lax.axis_size(chips), lax.axis_size(core))
    blocks = cut_along(array, dim, sizes[0] * sizes[1])
    inside = blocks.shape[1:]
    blocks = blocks.reshape(*sizes, *inside).swapaxes(0, 1).reshape(-1, *inside)
    blocks = lax.psum_scatter(blocks, core, scatter_dimension=0, tiled=True)
    return lax.psum_scatter(blocks, chips, scatter_dimension=0, tiled=True)[0]


def one_axis_at_a_time(array, axes):
    return functools.reduce(lax.psum, axes, array)


def reduce_rows(layer_acts, layer_grads):
    grad_own = scatter_pairs(
        jnp.einsum("ltr,ltc->rlc", layer_acts, layer_grads, preferred_element_type=jnp.float32),
        ("dp_0", "dp_1"),
        "dp_2",
        0,
    )
    partial_value = jnp.sum(grad_own * grad_own)
    return (grad_own, partial_value)


def adam_update(grad_own, master, first_moment, second_moment, clip_factor):
    clipped = clip_factor * grad_own
    new_first = beta_first * first_moment + (1.0 - beta_first) * clipped
    new_second = beta_second * second_moment + (1.0 - beta_second) * clipped * clipped
    step_dir = new_first / first_fix / (jnp.sqrt(new_second / second_fix) + epsilon)
    new_master = master - learn_rate * (step_dir + decay_rate * master)
    return (new_master, new_first, new_second)


def on_device(activations, out_grads, master, first_moment, second_moment):
    own_rows = master.shape[0]
    grad_own, layer_sum = reduce_rows(activations, out_grads)
    sum_squares = one_axis_at_a_time(layer_sum, TP_DP)
    entries = own_rows * lax.axis_size(TP) * lax.axis_size(DP) * master.shape[1] * master.shape[2]
    limit = limit_scale * math.sqrt(entries)
    clip_factor = limit / jnp.maximum(jnp.sqrt(sum_squares), limit)
    new_master, new_first, new_second = adam_update(
        grad_own, master, first_moment, second_moment, clip_factor
    )
    rounded = new_master.astype(jnp.bfloat16)
    tp_rows = lax.all_gather(rounded, DP, axis=0, tiled=True)
    return (new_master, new_first, new_second, tp_rows)


def solution(mesh):
    finer = Mesh(mesh.devices.reshape(4, 2, 4, 2, 2), ("tp_0", "tp_1", "dp_0", "dp_1", "dp_2"))
    in_specs = (
        P(None, DP, TP),
        P(None, DP, None),
        P(TP_DP, None, None),
        P(TP_DP, None, None),
        P(TP_DP, None, None),
    )
    out_specs = (
        P(TP_DP, None, None),
        P(TP_DP, None, None),
        P(TP_DP, None, None),
        P(TP, None, None),
    )
    return jax.shard_map(
        on_device, mesh=finer, in_specs=in_specs, out_specs=out_specs, check_vma=False
    )
```

profile of v0, /device:TPU:1, one launch (start us, length us, event | category | flops | bytes accessed | tf_op | source)
XLA Modules:
  0.0 349.5 jit_solution(12573614637732273600)
XLA Ops:
  7.2 0.0 reduce-scatter.3.cloned.1.call-start
  7.2 15.8 %fusion.5 = f32[2,2048,1024]{1,2,0:T(8,128)} fusion(bf16[2,1024,2048]{2,1,0:T(8,128)(2,1)} %param.6, bf16[2,1024,1024]{2,1,0:T(8,128)(2,1)} %param.5), kind=kOutput, calls=%fused_computation.9 | convolution fusion | flops 8589934592 | bytes 29360128 | tf_op jit(solution)/shard_map/ltr,ltc->rlc/dot_general | solution.py:46
  23.0 11.6 %copy.13 = f32[2,8,64,2,2048]{4,2,3,1,0:T(8,128)} copy(f32[2,8,64,2,2048]{4,2,0,1,3:T(8,128)} %bitcast.16) | data formatting | bytes 33554432 | tf_op jit(solution)/shard_map/transpose | solution.py:35
  34.7 0.0 reduce-scatter.3.cloned.1.call-update
  34.7 0.0 reduce-scatter.5.cloned.1.call-start
  34.7 31.5 %reduce-scatter.3.cloned.1.call-done = f32[8,64,2,2048]{3,1,2,0:T(8,128)} async-done(((f32[16,64,2,2048]{3,1,2,0:T(8,128)}), f32[8,64,2,2048]{3,1,2,0:T(8,128)}) %reduce-scatter.3.cloned.1.call-update) | async-done | bytes 8388624 | tf_op jit(solution)/shard_map/reduce_scatter | solution.py:36
  66.2 0.0 reduce-scatter.5.cloned.1.call-update
  66.2 0.0 all-gather.2.cloned.1.call-start
  66.3 172.5 %reduce-scatter.5.cloned.1.call-done = f32[1,64,2,2048]{3,1,2,0:T(8,128)} async-done(((f32[8,64,2,2048]{3,1,2,0:T(8,128)}), f32[1,64,2,2048]{3,1,2,0:T(8,128)}) %reduce-scatter.5.cloned.1.call-update) | async-done | bytes 1048592 | tf_op jit(solution)/shard_map/reduce_scatter | solution.py:37
  238.8 2.1 multiply_reduce_fusion
  240.9 9.1 %psum.35 = f32[]{:T(128)} all-reduce(f32[]{:T(128)} %multiply_reduce_fusion), channel_id=1, replica_groups=mesh['tp_0'=4,'tp_1'=2,'dp_0'=4,'dp_1'=2,'dp_2'=2] {'tp_0'}, use_global_device_ids=true, to_apply=%region_3.0 | all-reduce | flops 1 | bytes 8 | tf_op jit(solution)/shard_map/psum | solution.py:41
  250.0 5.9 %psum.36 = f32[]{:T(128)} all-reduce(f32[]{:T(128)} %psum.35), channel_id=1, replica_groups=mesh['tp_0'=4,'tp_1'=2,'dp_0'=4,'dp_1'=2,'dp_2'=2] {'tp_1'}, use_global_device_ids=true, to_apply=%region_4.0 | all-reduce | flops 1 | bytes 8 | tf_op jit(solution)/shard_map/psum | solution.py:41
  255.8 9.3 %psum.37 = f32[]{:T(128)} all-reduce(f32[]{:T(128)} %psum.36), channel_id=1, replica_groups=mesh['tp_0'=4,'tp_1'=2,'dp_0'=4,'dp_1'=2,'dp_2'=2] {'dp_0'}, use_global_device_ids=true, to_apply=%region_5.0 | all-reduce | flops 1 | bytes 8 | tf_op jit(solution)/shard_map/psum | solution.py:41
  265.1 4.4 %psum.38 = f32[]{:T(128)} all-reduce(f32[]{:T(128)} %psum.37), channel_id=1, replica_groups=mesh['tp_0'=4,'tp_1'=2,'dp_0'=4,'dp_1'=2,'dp_2'=2] {'dp_1'}, use_global_device_ids=true, to_apply=%region_6.0 | all-reduce | flops 1 | bytes 8 | tf_op jit(solution)/shard_map/psum | solution.py:41
  269.5 10.0 %psum.39 = f32[]{:T(128)} all-reduce(f32[]{:T(128)} %psum.38), channel_id=1, replica_groups=mesh['tp_0'=4,'tp_1'=2,'dp_0'=4,'dp_1'=2,'dp_2'=2] {'dp_2'}, use_global_device_ids=true, to_apply=%region_7.0 | all-reduce | flops 1 | bytes 8 | tf_op jit(solution)/shard_map/psum | solution.py:41
  280.3 4.5 %fusion.2 = (bf16[64,2,2048]{2,0,1:T(8,128)(2,1)S(1)}, f32[64,2,2048]{2,0,1:T(8,128)S(1)}, f32[64,2,2048]{2,0,1:T(8,128)S(1)}, f32[64,2,2048]{2,0,1:T(8,128)S(1)}) fusion(f32[64,2,2048]{2,1,0:T(2,128)} %param.7, f32[1,64,2,2048]{3,1,2,0:T(8,128)} %reduce-scatter.5.cloned.1.call-done, f32[]{:T(128)S(6)} %div.18, f32[64,2,2048]{2,1,0:T(2,128)} %param.8, ...), kind=kLoop, calls=%fused_computation.8 | loop fusion | flops 4456448 | bytes 7864324 | tf_op jit(solution)/shard_map/convert_element_type | solution.py:74
  284.8 1.3 copy.17
  286.1 0.0 all-gather.2.cloned.1.call-update
  286.1 1.8 copy.18
  287.9 1.8 copy.19
  289.7 1.8 copy.20
  291.5 43.5 %all-gather.2.cloned.1.call-done = bf16[1024,2,2048]{2,1,0:T(2,128)(2,1)} async-done(((bf16[64,2,2048]{2,1,0:T(2,128)(2,1)}), bf16[1024,2,2048]{2,1,0:T(2,128)(2,1)}) %all-gather.2.cloned.1.call-update) | async-done | bytes 8388624 | tf_op jit(solution)/shard_map/all_gather | solution.py:75
  335.0 8.0 %copy.33 = bf16[1024,2,2048]{2,1,0:T(2,128)(2,1)} copy(bf16[1024,2,2048]{2,1,0:T(2,128)(2,1)} %all-gather.2.cloned.1.call-done) | data formatting | bytes 16777216
Async XLA Ops:
  7.2 59.0 %reduce-scatter.3.cloned.1.call-start = ((), (), s32[]{:S(2)}) async-start(), calls=%async_computation.2 | async-start | bytes 25165824 | tf_op jit(solution)/shard_map/reduce_scatter | solution.py:36
  34.7 204.1 %reduce-scatter.5.cloned.1.call-start = ((), (), s32[]{:S(2)}) async-start(), calls=%async_computation.3 | async-start | bytes 9437184 | tf_op jit(solution)/shard_map/reduce_scatter | solution.py:37
  66.2 268.8 %all-gather.2.cloned.1.call-start = ((), (), s32[]{:S(2)}) async-start(), calls=%async_computation.4 | async-start | bytes 8912896 | tf_op jit(solution)/shard_map/all_gather | solution.py:75
Sparse Core Ops, SparseCore 0:
  34.8 31.3 reduce-scatter.2
  68.6 170.1 reduce-scatter.4
  286.2 48.6 all-gather.1
where the time goes:
time: 350 us; the launch traced here: 349 us
  waiting for transfers between devices  248 us (71%)
  blocking collectives  38.6 us (11%)
  local copies, waits for them, and re-layouts  26.3 us (8%)
  matrix products  15.8 us (5%)
  between operations  14.5 us (4%)
  other arithmetic  6.61 us (2%)
    reduce_scatter x1, waiting for transfers between devices, scatter_pairs(): return lax.psum_scatter(blocks, chips, scatter_dimension=0, tiled=True)[0]  173 us
    all_gather x1, waiting for transfers between devices, on_device(): tp_rows = lax.all_gather(rounded, DP, axis=0, tiled=True)  43.5 us
    psum x5, blocking collectives, one_axis_at_a_time(): return functools.reduce(lax.psum, axes, array)  38.6 us
    reduce_scatter x1, waiting for transfers between devices, scatter_pairs(): blocks = lax.psum_scatter(blocks, core, scatter_dimension=0, tiled=True)  31.5 us
    dot_general x1, matrix products, reduce_rows(): jnp.einsum('ltr,ltc->rlc', layer_acts, layer_grads, preferred_element_typ...  15.8 us
    unnamed x4, local copies, waits for them, and re-layouts  13.3 us
    transpose x1, local copies, waits for them, and re-layouts, scatter_pairs(): blocks = blocks.reshape(*sizes, *inside).swapaxes(0, 1).reshape(-1, *inside)  11.6 us
  transfers between devices with their start and end apart: 3, of which 3 were waited for; matrix products, arithmetic and copies ran while one was open for 2% of the time, Pallas kernels for 0%

commit v1 on v0

v1 whole, which is shorter than its diff:
```python
import functools
import math

import jax
import jax.numpy as jnp
from jax import lax
from jax.experimental import pallas as pl
from jax.experimental.pallas import tpu as pltpu
from jax.sharding import Mesh
from jax.sharding import PartitionSpec as P

DP = ("dp_0", "dp_1", "dp_2")
TP_DP = ("tp_0", "tp_1", "dp_0", "dp_1", "dp_2")
TP = ("tp_0", "tp_1")
MESH = pl.DeviceIdType.MESH
F32 = jnp.float32
BF16 = jnp.bfloat16


beta_first = 0.9
beta_second = 0.95
first_fix = 1.0 - 0.9**10
second_fix = 1.0 - 0.95**10
learn_rate = 0.01
decay_rate = 0.1
epsilon = 1e-08
limit_scale = 2.0

OWN = 64
WIDE = 256
HALF = WIDE // 2
STEPS = 8
LANES = 128
GATHERS = 4
X_ROWS = 288
Z_ROWS = 224
SUB = 32
TOP = 2.0**120
TINY = 1e-37


def encode(value):
    square = value * value
    fourth = square * square
    return (fourth * (square * (value * jnp.abs(value)))).astype(BF16)


def decode(code):
    power = code.astype(F32)
    half = lax.rsqrt(jnp.maximum(jnp.abs(power), TINY))
    eighth = lax.rsqrt(lax.rsqrt(half))
    return (power * half) * (eighth * (eighth * eighth))


def kernel(
    acts_hbm, grads_hbm, master_hbm, first_hbm, second_hbm,
    master_out, first_out, second_out, weights_out,
    acts, turned, outs, master, first, second, own_grad,
    pair_send, pair_recv, total,
    x1_send, x1_recv, xz1_send, xz1_recv, xz2_send, xz2_recv,
    zz1_send, zz1_recv, zz2_send, zz2_recv, zx_send, zx_recv,
    bound, bounds, norm_dp, norm_tp,
    load_sem, out_sem, state_sem, pair_ssem, pair_rsem, x1_ssem, x1_rsem, xz1_ssem, xz1_rsem, xz2_ssem, xz2_rsem,
    zz1_ssem, zz1_rsem, zz2_ssem, zz2_rsem, zx_ssem, zx_rsem,
    bound_ssem, bound_rsem, ndp_ssem, ndp_rsem, ntp_ssem, ntp_rsem,
    gx_ssem, gx_rsem, gz_ssem, gz_rsem, gd_ssem, gd_rsem,
):
    ny, nh = lax.axis_size("tp_0"), lax.axis_size("tp_1")
    y, h = lax.axis_index("tp_0"), lax.axis_index("tp_1")
    z, x, c = lax.axis_index("dp_0"), lax.axis_index("dp_1"), lax.axis_index("dp_2")
    nt = ny * nh
    dp_me = z * 4 + x * 2 + c
    tp_me = y * nh + h
    za, zb, zo = lax.rem(z + 1, 4), lax.rem(z + 3, 4), lax.rem(z + 2, 4)
    xo = 1 - x
    tokens = acts_hbm.shape[1]
    to_core = {"dp_2": 1 - c}
    to_x = {"dp_1": xo}
    to_za = {"dp_0": za}
    to_zb = {"dp_0": zb}

    def dp_of(k):
        other = lax.rem(dp_me + k, 16)
        return other, {"dp_0": other // 4, "dp_1": lax.rem(other // 2, 2), "dp_2": lax.rem(other, 2)}

    def tp_of(k):
        other = lax.rem(tp_me + k, nt)
        return other, {"tp_0": other // nh, "tp_1": lax.rem(other, nh)}

    def remote(src, dst, ssem, rsem, device):
        return pltpu.make_async_remote_copy(
            src_ref=src, dst_ref=dst, send_sem=ssem, recv_sem=rsem, device_id=device, device_id_type=MESH
        )

    def acts_load(l):
        return pltpu.make_async_copy(acts_hbm.at[l], acts.at[l], load_sem.at[l])

    def outs_load(i):
        return pltpu.make_async_copy(
            grads_hbm.at[i // 4, :, pl.ds(pl.multiple_of(lax.rem(i, 4) * (2 * WIDE), 2 * WIDE), 2 * WIDE)],
            outs.at[i],
            out_sem.at[i],
        )

    states = (
        pltpu.make_async_copy(master_hbm, master, state_sem.at[0]),
        pltpu.make_async_copy(first_hbm, first, state_sem.at[1]),
        pltpu.make_async_copy(second_hbm, second, state_sem.at[2]),
    )
    acts_load(0).start()
    outs_load(0).start()
    acts_load(1).start()

    def start_outs(i, carry):
        outs_load(i).start()
        return carry

    lax.fori_loop(1, STEPS, start_outs, 0)
    for copy in states:
        copy.start()

    barrier = pltpu.get_barrier_semaphore()

    def greet_dp(k, carry):
        pl.semaphore_signal(barrier, inc=1, device_id=dp_of(k)[1], device_id_type=MESH)
        return carry

    def greet_tp(k, carry):
        pl.semaphore_signal(barrier, inc=1, device_id=tp_of(k)[1], device_id_type=MESH)
        return carry

    lax.fori_loop(1, 16, greet_dp, 0)
    lax.fori_loop(1, nt, greet_tp, 0)

    def turn(l):
        for q in range(8):
            flipped = acts[l, :, q * LANES : (q + 1) * LANES].T
            turned[l, 0, q * OWN : (q + 1) * OWN, :] = flipped[:OWN]
            turned[l, 1, q * OWN : (q + 1) * OWN, :] = flipped[OWN:]

    def largest(ref, lead):
        rows, wide = ref.shape[1], ref.shape[2]

        def step(r, best):
            part = jnp.abs(ref[lead, pl.ds(pl.multiple_of(r * 64, 64), 64), :])
            return jnp.maximum(best, jnp.max(part.reshape(4, 16, wide), axis=0))

        return lax.fori_loop(0, rows // 64, step, jnp.zeros((16, wide), BF16))

    acts_load(0).wait()
    turn(0)

    def product(l, core, i, p):
        return jnp.dot(
            turned[l, core], outs[i, :, p * WIDE : (p + 1) * WIDE], preferred_element_type=F32
        ).reshape(8, OWN, WIDE)

    def pair_copy(i, p):
        slot = lax.rem(i, 2)
        return remote(
            pair_send.at[slot, p], pair_recv.at[i, p], pair_ssem.at[slot, p], pair_rsem.at[i, p], to_core
        )

    def multiply(i):
        l = i // 4

        @pl.when(i >= 2)
        def _():
            for p in range(2):
                pair_copy(i - 2, p).wait_send()

        slot = lax.rem(i, 2)
        pair_send[slot, 0] = product(l, 1 - c, i, 0)
        pair_send[slot, 1] = product(l, 1 - c, i, 1)
        pair_copy(i, 0).start()
        total[i, 0] = product(l, c, i, 0)
        pair_copy(i, 1).start()
        total[i, 1] = product(l, c, i, 1)

    outs_load(0).wait()
    pl.semaphore_wait(barrier, 15 + nt - 1)
    multiply(0)

    acts_load(1).wait()
    biggest_act = jnp.maximum(jnp.max(largest(acts, 0).astype(F32)), jnp.max(largest(acts, 1).astype(F32)))
    best = largest(outs, 0)

    def widen(i, best):
        outs_load(i).wait()
        return jnp.maximum(best, largest(outs, i))

    best = lax.fori_loop(1, STEPS, widen, best)
    biggest_out = jnp.max(best.astype(F32))
    own_bound = jnp.maximum(biggest_act * biggest_out * (1.01 * tokens), 1e-30)
    bounds[dp_me] = jnp.full((8, LANES), own_bound, F32)
    bound[...] = jnp.full((8, LANES), own_bound, F32)

    def bound_copy(k):
        return remote(bound, bounds.at[dp_me], bound_ssem.at[k], bound_rsem.at[dp_me], dp_of(k)[1])

    def bound_send(k, carry):
        bound_copy(k).start()
        return carry

    lax.fori_loop(1, 16, bound_send, 0)
    turn(1)

    def bound_wait(other):
        remote(bound, bounds.at[other], bound_ssem.at[0], bound_rsem.at[other], to_core).wait_recv()

    bound_wait(z * 4 + x * 2 + 1 - c)

    top = TOP ** 0.125
    chip_bound = (bounds[dp_me] + bounds[z * 4 + x * 2 + 1 - c])[0:1, 0:1]
    chip_scale = top / chip_bound

    def paired(i, p, q):
        return total[i, p, q] + pair_recv[i, p, q]

    def x1_copy(i):
        return remote(x1_send.at[i], x1_recv.at[i], x1_ssem.at[i], x1_rsem.at[i], to_x)

    def z_copies(send, recv, ssem, rsem, i):
        return (
            remote(send.at[i, 0], recv.at[i, 0], ssem.at[i, 0], rsem.at[i, 0], to_za),
            remote(send.at[i, 1], recv.at[i, 1], ssem.at[i, 1], rsem.at[i, 1], to_zb),
        )

    def xz1_copies(i):
        return z_copies(xz1_send, xz1_recv, xz1_ssem, xz1_rsem, i)

    def xz2_copies(i):
        return z_copies(xz2_send, xz2_recv, xz2_ssem, xz2_rsem, i)

    def zz1_copies(i):
        return z_copies(zz1_send, zz1_recv, zz1_ssem, zz1_rsem, i)

    def zz2_copies(i):
        return z_copies(zz2_send, zz2_recv, zz2_ssem, zz2_rsem, i)

    def zx_copy(i):
        return remote(zx_send.at[i], zx_recv.at[i], zx_ssem.at[i], zx_rsem.at[i], to_x)

    lo, hi = slice(0, HALF), slice(HALF, WIDE)

    def stage_one(i):
        pair_copy(i, 0).wait_recv()
        for zz in range(4):
            x1_send[i, zz] = encode(paired(i, 0, zz * 2 + xo) * chip_scale)
        x1_copy(i).start()
        pair_copy(i, 1).wait_recv()
        for xx in range(2):
            far = encode(paired(i, 1, zo * 2 + xx) * chip_scale)
            zz1_send[i, 0, 0, xx] = far[:, lo]
            zz1_send[i, 1, 0, xx] = far[:, hi]
            q = za * 2 + xx
            zz1_send[i, 0, 1, xx] = encode((total[i, 1, q, :, hi] + pair_recv[i, 1, q, :, hi]) * chip_scale)
            q = zb * 2 + xx
            zz1_send[i, 1, 1, xx] = encode((total[i, 1, q, :, lo] + pair_recv[i, 1, q, :, lo]) * chip_scale)
        for copy in zz1_copies(i):
            copy.start()

    def first_loop(i, carry):
        multiply(i)
        stage_one(i - 1)
        return carry

    lax.fori_loop(1, STEPS, first_loop, 0)
    stage_one(STEPS - 1)

    def bound_rest(k, carry):
        other = lax.rem(dp_me + k, 16)

        @pl.when(other != z * 4 + x * 2 + 1 - c)
        def _():
            bound_wait(other)

        return carry

    lax.fori_loop(1, 16, bound_rest, 0)

    def bound_of(zz, xx):
        return (bounds[zz * 4 + xx * 2] + bounds[zz * 4 + xx * 2 + 1])[0:1, 0:1]

    from_x = bound_of(z, xo) * (1.0 / top)
    from_zb = bound_of(zb, x) * (1.0 / top)
    from_za = bound_of(za, x) * (1.0 / top)
    whole = jnp.sum(bounds[...], axis=0)[0:1, 0:1] * 1.01
    scale = top / whole
    unscale = whole * (1.0 / top)

    def stage_two(i):
        x1_copy(i).wait_recv()
        for zz in range(4):
            q = zz * 2 + x
            total[i, 0, q] = paired(i, 0, q) + decode(x1_recv[i, zz]) * from_x
        far = encode(total[i, 0, zo * 2 + x] * scale)
        xz1_send[i, 0, 0] = far[:, lo]
        xz1_send[i, 1, 0] = far[:, hi]
        xz1_send[i, 0, 1] = encode(total[i, 0, za * 2 + x, :, hi] * scale)
        xz1_send[i, 1, 1] = encode(total[i, 0, zb * 2 + x, :, lo] * scale)
        for copy in xz1_copies(i):
            copy.start()
        for copy in zz1_copies(i):
            copy.wait_recv()
        for xx in range(2):
            q = za * 2 + xx
            mine = total[i, 1, q, :, lo] + pair_recv[i, 1, q, :, lo]
            zz2_send[i, 0, xx] = encode((mine + decode(zz1_recv[i, 0, 0, xx]) * from_zb) * scale)
            q = zb * 2 + xx
            mine = total[i, 1, q, :, hi] + pair_recv[i, 1, q, :, hi]
            zz2_send[i, 1, xx] = encode((mine + decode(zz1_recv[i, 1, 0, xx]) * from_za) * scale)
        for copy in zz2_copies(i):
            copy.start()

    def stage_three(i):
        for copy in zz2_copies(i):
            copy.wait_recv()

        def summed(xx):
            q = z * 2 + xx
            low = (
                total[i, 1, q, :, lo] + pair_recv[i, 1, q, :, lo]
                + decode(zz1_recv[i, 1, 1, xx]) * from_za + decode(zz2_recv[i, 0, xx]) * unscale
            )
            high = (
                total[i, 1, q, :, hi] + pair_recv[i, 1, q, :, hi]
                + decode(zz1_recv[i, 0, 1, xx]) * from_zb + decode(zz2_recv[i, 1, xx]) * unscale
            )
            return low, high

        low, high = summed(xo)
        zx_send[i, :, lo] = encode(low * scale)
        zx_send[i, :, hi] = encode(high * scale)
        zx_copy(i).start()
        for copy in xz1_copies(i):
            copy.wait_recv()
        xz2_send[i, 0] = encode(total[i, 0, za * 2 + x, :, lo] * scale + decode(xz1_recv[i, 0, 0]))
        xz2_send[i, 1] = encode(total[i, 0, zb * 2 + x, :, hi] * scale + decode(xz1_recv[i, 1, 0]))
        for copy in xz2_copies(i):
            copy.start()
        low, high = summed(x)
        total[i, 1, z * 2 + x, :, lo] = low
        total[i, 1, z * 2 + x, :, hi] = high

    def put(i, j, value):
        base = (lax.rem(i, 4) * 4 + j) * 2 + i // 4
        for r in range(OWN // 8):
            own_grad[pl.ds(base + r * 8 * 32, 8, stride=32), :] = value[r * 8 : (r + 1) * 8]
        return jnp.sum((value * value).reshape(OWN // 8, 8, LANES), axis=0)

    def final(i, squares):
        for copy in xz2_copies(i):
            copy.wait_recv()
        q = z * 2 + x
        g = total[i, 0, q, :, lo] + (decode(xz1_recv[i, 1, 1]) + decode(xz2_recv[i, 0])) * unscale
        squares = squares + put(i, 0, g)
        g = total[i, 0, q, :, hi] + (decode(xz1_recv[i, 0, 1]) + decode(xz2_recv[i, 1])) * unscale
        squares = squares + put(i, 1, g)
        zx_copy(i).wait_recv()
        g = total[i, 1, q] + decode(zx_recv[i]) * unscale
        squares = squares + put(i, 2, g[:, lo])
        return squares + put(i, 3, g[:, hi])

    stage_two(0)
    stage_two(1)
    stage_three(0)

    def second_loop(i, squares):
        stage_two(i)
        stage_three(i - 1)
        return final(i - 2, squares)

    squares = lax.fori_loop(2, STEPS, second_loop, jnp.zeros((8, LANES), F32))
    stage_three(STEPS - 1)
    squares = final(STEPS - 2, squares)
    squares = final(STEPS - 1, squares)

    norm_dp[dp_me] = squares

    def ndp_copy(k, slot):
        return remote(norm_dp.at[slot], norm_dp.at[slot], ndp_ssem.at[k], ndp_rsem.at[slot], dp_of(k)[1])

    def ntp_copy(k, slot):
        return remote(norm_tp.at[slot], norm_tp.at[slot], ntp_ssem.at[k], ntp_rsem.at[slot], tp_of(k)[1])

    def exchange(copy, count, me):
        def send(k, carry):
            copy(k, me).start()
            return carry

        def receive(k, carry):
            copy(k, lax.rem(me + k, count)).wait_recv()
            return carry

        lax.fori_loop(1, count, send, 0)
        lax.fori_loop(1, count, receive, 0)

    exchange(ndp_copy, 16, dp_me)
    norm_tp[tp_me] = jnp.sum(norm_dp[...], axis=0)
    for copy in states:
        copy.wait()
    exchange(ntp_copy, nt, tp_me)
    sum_squares = jnp.sum(jnp.sum(norm_tp[...], axis=0), keepdims=True)
    entries = OWN * 16 * nt * 2 * 2048
    limit = limit_scale * math.sqrt(entries)
    clip_factor = limit / jnp.maximum(jnp.sqrt(sum_squares), limit)

    def update(start):
        rows = pl.ds(pl.multiple_of(start, SUB), SUB)
        clipped = clip_factor * own_grad[rows, :]
        new_first = beta_first * first[rows, :] + (1.0 - beta_first) * clipped
        new_second = beta_second * second[rows, :] + (1.0 - beta_second) * clipped * clipped
        step_dir = new_first * (1.0 / first_fix) / (jnp.sqrt(new_second * (1.0 / second_fix)) + epsilon)
        old = master[rows, :]
        new_master = old - learn_rate * (step_dir + decay_rate * old)
        first_out[rows, :] = new_first
        second_out[rows, :] = new_second
        master_out[rows, :] = new_master
        weights_out[dp_me, rows, :] = new_master.astype(BF16)

    def x_part(k):
        return pl.ds(pl.multiple_of(k * X_ROWS, 16), X_ROWS)

    def z_part(k):
        return pl.ds(pl.multiple_of(GATHERS * X_ROWS + k * Z_ROWS, 16), Z_ROWS)

    def x_half(k, n):
        return pl.ds(pl.multiple_of(k * X_ROWS + n * (X_ROWS // 2), 16), X_ROWS // 2)

    def z_half(k, n):
        return pl.ds(pl.multiple_of(GATHERS * X_ROWS + k * Z_ROWS + n * (Z_ROWS // 2), 16), Z_ROWS // 2)

    def move(zz, xx, rows, ssem, rsem, device):
        place = weights_out.at[zz * 4 + xx * 2 + c, rows, :]
        return remote(place, place, ssem, rsem, device)

    def gx(k, n, zz, xx, rows):
        return move(zz, xx, rows, gx_ssem.at[k, n], gx_rsem.at[k, n], to_x)

    def gz(k, n, zz, xx, rows, device):
        return move(zz, xx, rows, gz_ssem.at[k, n], gz_rsem.at[k, n], device)

    def gd(zz, xx, rows):
        return move(zz, xx, rows, gd_ssem, gd_rsem, to_core)

    def x_own(k, xx):
        return gx(k, 0, z, xx, x_part(k))

    def z_cross(k, n, zz, xx):
        return gx(k, 1 + n, zz, xx, z_part(k))

    def x_spread(k, xx, zz_a, zz_b, n):
        return (
            gz(k, n, zz_a, xx, x_part(k), to_za),
            gz(k, n + 1, zz_b, xx, x_part(k), to_zb),
        )

    def x_halves(k, xx, zz_a, zz_b, n):
        return (
            gz(k, n, zz_a, xx, x_half(k, 0), to_za),
            gz(k, n + 1, zz_b, xx, x_half(k, 1), to_zb),
        )

    def z_spread(k, zz_a, zz_b):
        return (
            gz(k, 8, zz_a, x, z_part(k), to_za),
            gz(k, 9, zz_b, x, z_part(k), to_zb),
        )

    def z_halves(k, zz_a, zz_b):
        return (
            gz(k, 10, zz_a, x, z_half(k, 0), to_za),
            gz(k, 11, zz_b, x, z_half(k, 1), to_zb),
        )

    def update_loop(k, carry):
        def in_x(s, carry):
            update(k * X_ROWS + s * SUB)
            return carry

        def in_z(s, carry):
            update(GATHERS * X_ROWS + k * Z_ROWS + s * SUB)
            return carry

        lax.fori_loop(0, X_ROWS // SUB, in_x, 0)
        x_own(k, x).start()
        gd(z, x, x_part(k)).start()
        lax.fori_loop(0, Z_ROWS // SUB, in_z, 0)
        for copy in z_spread(k, z, z):
            copy.start()
        gd(z, x, z_part(k)).start()
        return carry

    lax.fori_loop(0, GATHERS, update_loop, 0)

    def own_loop(k, carry):
        z_cross(k, 0, z, x).start()
        for copy in x_spread(k, x, z, z, 0):
            copy.start()
        return carry

    lax.fori_loop(0, GATHERS, own_loop, 0)

    def hop_one(k):
        x_own(k, xo).wait_recv()
        for copy in x_spread(k, xo, z, z, 2):
            copy.start()
        gd(z, xo, x_part(k)).start()
        from_below, from_above = z_spread(k, zb, za)
        halves = z_halves(k, zb, za)
        from_below.wait_recv()
        halves[0].start()
        z_cross(k, 1, zb, x).start()
        gd(zb, x, z_part(k)).start()
        from_above.wait_recv()
        halves[1].start()
        z_cross(k, 2, za, x).start()
        gd(za, x, z_part(k)).start()

    def hop_two(k):
        for xx, n in ((x, 0), (xo, 2)):
            from_below, from_above = x_spread(k, xx, zb, za, n)
            halves = x_halves(k, xx, zb, za, 4 + n)
            from_below.wait_recv()
            halves[0].start()
            gd(zb, xx, x_part(k)).start()
            from_above.wait_recv()
            halves[1].start()
            gd(za, xx, x_part(k)).start()
        for copy in z_halves(k, zo, zo):
            copy.wait_recv()
        z_cross(k, 3, zo, x).start()
        gd(zo, x, z_part(k)).start()

    def hop_three(k):
        for n, zz in ((0, z), (1, zb), (2, za), (3, zo)):
            z_cross(k, n, zz, xo).wait_recv()
            gd(zz, xo, z_part(k)).start()
        for xx, n in ((x, 0), (xo, 2)):
            for copy in x_halves(k, xx, zo, zo, 4 + n):
                copy.wait_recv()
            gd(zo, xx, x_part(k)).start()

    hop_one(0)
    hop_one(1)
    hop_two(0)

    def gather_loop(k, carry):
        hop_one(k)
        hop_two(k - 1)
        hop_three(k - 2)
        return carry

    lax.fori_loop(2, GATHERS, gather_loop, 0)
    hop_two(GATHERS - 1)
    hop_three(GATHERS - 2)
    hop_three(GATHERS - 1)

    def drain_steps(i, carry):
        x1_copy(i).wait_send()
        zx_copy(i).wait_send()
        for copies in (xz1_copies, xz2_copies, zz1_copies, zz2_copies):
            for copy in copies(i):
                copy.wait_send()
        return carry

    def drain_gather(k, carry):
        x_own(k, x).wait_send()
        for n in range(4):
            z_cross(k, n, z, x).wait_send()
        for n in (0, 2):
            for copy in x_spread(k, x, z, z, n) + x_halves(k, x, z, z, 4 + n):
                copy.wait_send()
        for copy in z_spread(k, z, z) + z_halves(k, z, z):
            copy.wait_send()
        return carry

    def drain_dp(k, carry):
        bound_copy(k).wait_send()
        ndp_copy(k, dp_me).wait_send()
        return carry

    def drain_tp(k, carry):
        ntp_copy(k, tp_me).wait_send()
        return carry

    for i in (STEPS - 2, STEPS - 1):
        for p in range(2):
            pair_copy(i, p).wait_send()
    lax.fori_loop(0, STEPS, drain_steps, 0)
    lax.fori_loop(0, GATHERS, drain_gather, 0)
    lax.fori_loop(1, 16, drain_dp, 0)
    lax.fori_loop(1, nt, drain_tp, 0)
    everything = weights_out.at[pl.ds(0, 8)]
    passed = remote(everything, everything, gd_ssem, gd_rsem, to_core)
    passed.wait_send()
    passed.wait_recv()


def fused(acts, grads, master, first, second):
    tokens = acts.shape[1]
    rows = OWN * 32
    dma = pltpu.SemaphoreType.DMA
    vmem = pltpu.VMEM
    scratch = [
        vmem((2, tokens, 1024), BF16),
        vmem((2, 2, 512, tokens), BF16),
        vmem((STEPS, tokens, 2 * WIDE), BF16),
        vmem((rows, LANES), F32),
        vmem((rows, LANES), F32),
        vmem((rows, LANES), F32),
        vmem((rows, LANES), F32),
        vmem((2, 2, 8, OWN, WIDE), F32),
        vmem((STEPS, 2, 8, OWN, WIDE), F32),
        vmem((STEPS, 2, 8, OWN, WIDE), F32),
    ]
    for shape in (
        (STEPS, 4, OWN, WIDE),
        (STEPS, 2, 2, OWN, HALF),
        (STEPS, 2, OWN, HALF),
        (STEPS, 2, 2, 2, OWN, HALF),
        (STEPS, 2, 2, OWN, HALF),
        (STEPS, OWN, WIDE),
    ):
        scratch += [vmem(shape, BF16), vmem(shape, BF16)]
    tp = lax.axis_size("tp_0") * lax.axis_size("tp_1")
    scratch += [
        vmem((8, LANES), F32),
        vmem((16, 8, LANES), F32),
        vmem((16, 8, LANES), F32),
        vmem((tp, 8, LANES), F32),
        dma((2,)), dma((STEPS,)), dma((3,)),
        dma((2, 2)), dma((STEPS, 2)),
        dma((STEPS,)), dma((STEPS,)),
        dma((STEPS, 2)), dma((STEPS, 2)),
        dma((STEPS, 2)), dma((STEPS, 2)),
        dma((STEPS, 2)), dma((STEPS, 2)),
        dma((STEPS, 2)), dma((STEPS, 2)),
        dma((STEPS,)), dma((STEPS,)),
        dma((16,)), dma((16,)),
        dma((16,)), dma((16,)),
        dma((tp,)), dma((tp,)),
        dma((GATHERS, 5)), dma((GATHERS, 5)),
        dma((GATHERS, 12)), dma((GATHERS, 12)),
        dma, dma,
    ]
    anywhere = pl.BlockSpec(memory_space=pl.ANY)
    inside = pl.BlockSpec(memory_space=pltpu.VMEM)
    return pl.pallas_call(
        kernel,
        out_shape=(
            jax.ShapeDtypeStruct((rows, LANES), F32),
            jax.ShapeDtypeStruct((rows, LANES), F32),
            jax.ShapeDtypeStruct((rows, LANES), F32),
            jax.ShapeDtypeStruct((16, rows, LANES), BF16),
        ),
        in_specs=[anywhere] * 5,
        out_specs=(inside,) * 4,
        scratch_shapes=scratch,
        compiler_params=pltpu.CompilerParams(
            collective_id=0, has_side_effects=True, vmem_limit_bytes=64 * 1024 * 1024 - 64 * 1024
        ),
    )(acts, grads, master, first, second)


def to_rows(array):
    own = array.shape[0]
    return array.reshape(own, 2, 16, LANES).swapaxes(1, 2).reshape(own * 32, LANES)


def from_rows(array):
    own = array.shape[0] // 32
    return array.reshape(own, 16, 2, LANES).swapaxes(1, 2).reshape(own, 2, 2048)


def on_device(activations, out_grads, master, first_moment, second_moment):
    new_master, new_first, new_second, weights = fused(
        activations, out_grads, to_rows(master), to_rows(first_moment), to_rows(second_moment)
    )
    return (
        from_rows(new_master),
        from_rows(new_first),
        from_rows(new_second),
        from_rows(weights.reshape(-1, LANES)),
    )


def solution(mesh):
    finer = Mesh(mesh.devices.reshape(4, 2, 4, 2, 2), ("tp_0", "tp_1", "dp_0", "dp_1", "dp_2"))
    in_specs = (
        P(None, DP, TP),
        P(None, DP, None),
        P(TP_DP, None, None),
        P(TP_DP, None, None),
        P(TP_DP, None, None),
    )
    out_specs = (
        P(TP_DP, None, None),
        P(TP_DP, None, None),
        P(TP_DP, None, None),
        P(TP, None, None),
    )
    return jax.shard_map(
        on_device, mesh=finer, in_specs=in_specs, out_specs=out_specs, check_vma=False
    )
```

time: 350 us -> 123 us (0.35)
  waiting for transfers between devices: 248 us -> 0 us
  Pallas kernels: 0 us -> 107 us
  blocking collectives: 38.6 us -> 0 us
  matrix products: 15.8 us -> 0 us
  between operations: 14.5 us -> 0.64 us
  local copies, waits for them, and re-layouts: 26.3 us -> 14.8 us
  other arithmetic: 6.61 us -> 0 us
    reduce_scatter x2 -> x0, waiting for transfers between devices: 204 us -> none  [the longest x1 173 us: scatter_pairs(): return lax.psum_scatter(blocks, chips, scatter_dimension=0, tiled=True)[0]]
    pallas_call x0 -> x1, Pallas kernels: none -> 107 us  [fused(): pl.pallas_call(kernel, out_shape=(jax.ShapeDtypeStruct((rows, LANES), F32...]
    all_gather x1 -> x0, waiting for transfers between devices: 43.5 us -> none  [on_device(): tp_rows = lax.all_gather(rounded, DP, axis=0, tiled=True)]
    psum x5 -> x0, blocking collectives: 38.6 us -> none  [one_axis_at_a_time(): return functools.reduce(lax.psum, axes, array)]
    dot_general x1 -> x0, matrix products: 15.8 us -> none  [reduce_rows(): jnp.einsum('ltr,ltc->rlc', layer_acts, layer_grads, preferred_element_typ...]
    transpose x1 -> x0, local copies, waits for them, and re-layouts: 11.6 us -> none  [scatter_pairs(): blocks = blocks.reshape(*sizes, *inside).swapaxes(0, 1).reshape(-1, *inside)]
    convert_element_type x1 -> x0, other arithmetic: 4.51 us -> none  [on_device(): rounded = new_master.astype(jnp.bfloat16)]
  transfers between devices with their start and end apart: 3 -> 0, of which waited for: 3 -> 0; matrix products, arithmetic and copies ran while one was open for 2% -> 0% of each run, Pallas kernels for 0% -> 0%
where the time goes in v1:
time: 123 us; the launch traced here: 122 us
  Pallas kernels  107 us (87%)
  local copies, waits for them, and re-layouts  14.8 us (12%)
    pallas_call x1, Pallas kernels, fused(): pl.pallas_call(kernel, out_shape=(jax.ShapeDtypeStruct((rows, LANES), F32...  107 us
    unnamed x4, local copies, waits for them, and re-layouts  14.8 us

profile of v1, /device:TPU:1, one launch (start us, length us, event | category | flops | bytes accessed | tf_op | source)
XLA Modules:
  0.0 122.4 jit_solution(2932257298007972879)
XLA Ops:
  0.6 107.0 %shard_map.84 = (f32[2048,128]{1,0:T(8,128)}, f32[2048,128]{1,0:T(8,128)}, f32[2048,128]{1,0:T(8,128)}, bf16[16,2048,128]{2,1,0:T(8,128)(2,1)}) custom-call(bf16[2,1024,1024]{2,1,0:T(8,128)(2,1)} %acts_hbm.1, bf16[2,1024,2048]{2,1,0:T(8,128)(2,1)} %grads_hbm.1, f32[2048,128]{1,0:T(8,128)} %bitcast.39, f32[2048,128]{1,0:T(8,128)} %bitcast.40, ...), custom_call_target="tpu_custom_call" | custom-call | tf_op jit(solution)/shard_map/pallas_call | solution.py:650
  107.6 2.3 %copy.20 = f32[64,2,2048]{2,1,0:T(2,128)} copy(f32[64,2,2048]{2,1,0:T(2,128)} %bitcast.38) | data formatting | bytes 2097152
  109.9 2.3 %copy.21 = f32[64,2,2048]{2,1,0:T(2,128)} copy(f32[64,2,2048]{2,1,0:T(2,128)} %bitcast.37) | data formatting | bytes 2097152
  112.2 2.3 %copy.22 = f32[64,2,2048]{2,1,0:T(2,128)} copy(f32[64,2,2048]{2,1,0:T(2,128)} %bitcast.36) | data formatting | bytes 2097152
  114.4 8.0 %copy.23 = bf16[1024,2,2048]{2,1,0:T(2,128)(2,1)} copy(bf16[1024,2,2048]{2,1,0:T(2,128)(2,1)} %bitcast.35) | data formatting | bytes 16777216

commit v2 on v1

--- a/solution.py
+++ b/solution.py
@@ -35,6 +35,9 @@
 X_ROWS = 288
 Z_ROWS = 224
 SUB = 32
+LAG_TWO = 5
+LAG_THREE = 8
+LAG_END = 12
 TOP = 2.0**120
 TINY = 1e-37
 
@@ -59,7 +62,7 @@
     pair_send, pair_recv, total,
     x1_send, x1_recv, xz1_send, xz1_recv, xz2_send, xz2_recv,
     zz1_send, zz1_recv, zz2_send, zz2_recv, zx_send, zx_recv,
-    bound, bounds, norm_dp, norm_tp,
+    bound, bounds, norm_dp, norm_tp, squares_ref,
     load_sem, out_sem, state_sem, pair_ssem, pair_rsem, x1_ssem, x1_rsem, xz1_ssem, xz1_rsem, xz2_ssem, xz2_rsem,
     zz1_ssem, zz1_rsem, zz2_ssem, zz2_rsem, zx_ssem, zx_rsem,
     bound_ssem, bound_rsem, ndp_ssem, ndp_rsem, ntp_ssem, ntp_rsem,
@@ -260,14 +263,6 @@
         for copy in zz1_copies(i):
             copy.start()
 
-    def first_loop(i, carry):
-        multiply(i)
-        stage_one(i - 1)
-        return carry
-
-    lax.fori_loop(1, STEPS, first_loop, 0)
-    stage_one(STEPS - 1)
-
     def bound_rest(k, carry):
         other = lax.rem(dp_me + k, 16)
 
@@ -277,19 +272,20 @@
 
         return carry
 
-    lax.fori_loop(1, 16, bound_rest, 0)
-
     def bound_of(zz, xx):
         return (bounds[zz * 4 + xx * 2] + bounds[zz * 4 + xx * 2 + 1])[0:1, 0:1]
 
-    from_x = bound_of(z, xo) * (1.0 / top)
-    from_zb = bound_of(zb, x) * (1.0 / top)
-    from_za = bound_of(za, x) * (1.0 / top)
-    whole = jnp.sum(bounds[...], axis=0)[0:1, 0:1] * 1.01
-    scale = top / whole
-    unscale = whole * (1.0 / top)
+    def scales():
+        whole = jnp.sum(bounds[...], axis=0)[0:1, 0:1] * 1.01
+        return top / whole, whole * (1.0 / top)
+
+    def from_z():
+        return bound_of(za, x) * (1.0 / top), bound_of(zb, x) * (1.0 / top)
 
     def stage_two(i):
+        scale, unscale = scales()
+        from_za, from_zb = from_z()
+        from_x = bound_of(z, xo) * (1.0 / top)
         x1_copy(i).wait_recv()
         for zz in range(4):
             q = zz * 2 + x
@@ -314,6 +310,8 @@
             copy.start()
 
     def stage_three(i):
+        scale, unscale = scales()
+        from_za, from_zb = from_z()
         for copy in zz2_copies(i):
             copy.wait_recv()
 
@@ -349,7 +347,9 @@
             own_grad[pl.ds(base + r * 8 * 32, 8, stride=32), :] = value[r * 8 : (r + 1) * 8]
         return jnp.sum((value * value).reshape(OWN // 8, 8, LANES), axis=0)
 
-    def final(i, squares):
+    def final(i):
+        unscale = scales()[1]
+        squares = squares_ref[...]
         for copy in xz2_copies(i):
             copy.wait_recv()
         q = z * 2 + x
@@ -360,21 +360,29 @@
         zx_copy(i).wait_recv()
         g = total[i, 1, q] + decode(zx_recv[i]) * unscale
         squares = squares + put(i, 2, g[:, lo])
-        return squares + put(i, 3, g[:, hi])
-
-    stage_two(0)
-    stage_two(1)
-    stage_three(0)
-
-    def second_loop(i, squares):
-        stage_two(i)
-        stage_three(i - 1)
-        return final(i - 2, squares)
-
-    squares = lax.fori_loop(2, STEPS, second_loop, jnp.zeros((8, LANES), F32))
-    stage_three(STEPS - 1)
-    squares = final(STEPS - 2, squares)
-    squares = final(STEPS - 1, squares)
+        squares_ref[...] = squares + put(i, 3, g[:, hi])
+
+    def turn_of(t, squares):
+        def during(first, last, work, argument):
+            @pl.when((t >= first) & (t < last))
+            def _():
+                work(argument)
+
+        during(1, STEPS, multiply, t)
+        during(1, STEPS + 1, stage_one, t - 1)
+
+        @pl.when(t == LAG_TWO)
+        def _():
+            lax.fori_loop(1, 16, bound_rest, 0)
+
+        during(LAG_TWO, LAG_TWO + STEPS, stage_two, t - LAG_TWO)
+        during(LAG_THREE, LAG_THREE + STEPS, stage_three, t - LAG_THREE)
+        during(LAG_END, LAG_END + STEPS, final, t - LAG_END)
+        return squares
+
+    squares_ref[...] = jnp.zeros((8, LANES), F32)
+    lax.fori_loop(1, LAG_END + STEPS, turn_of, 0)
+    squares = squares_ref[...]
 
     norm_dp[dp_me] = squares
 
@@ -630,6 +638,7 @@
         vmem((16, 8, LANES), F32),
         vmem((16, 8, LANES), F32),
         vmem((tp, 8, LANES), F32),
+        vmem((8, LANES), F32),
         dma((2,)), dma((STEPS,)), dma((3,)),
         dma((2, 2)), dma((STEPS, 2)),
         dma((STEPS,)), dma((STEPS,)),
@@ -650,18 +659,42 @@
     return pl.pallas_call(
         kernel,
         out_shape=(
-            jax.ShapeDtypeStruct((rows, LANES), F32),
-            jax.ShapeDtypeStruct((rows, LANES), F32),
-            jax.ShapeDtypeStruct((rows, LANES), F32),
-            jax.ShapeDtypeStruct((16, rows, LANES), BF16),
+            vmem((rows, LANES), F32),
+            vmem((rows, LANES), F32),
+            vmem((rows, LANES), F32),
+            vmem((16, rows, LANES), BF16),
         ),
         in_specs=[anywhere] * 5,
         out_specs=(inside,) * 4,
         scratch_shapes=scratch,
         compiler_params=pltpu.CompilerParams(
-            collective_id=0, has_side_effects=True, vmem_limit_bytes=64 * 1024 * 1024 - 64 * 1024
+            collective_id=0, has_side_effects=True, vmem_limit_bytes=50 * 1024 * 1024
         ),
     )(acts, grads, master, first, second)
+
+
+def store_kernel(master, first, second, weights, master_out, first_out, second_out, weights_out, sems):
+    copies = [
+        pltpu.make_async_copy(weights.at[pl.ds(4 * n, 4)], weights_out.at[pl.ds(4 * n, 4)], sems.at[n])
+        for n in range(4)
+    ]
+    for n, (value, out) in enumerate(((master, master_out), (first, first_out), (second, second_out))):
+        copies.append(pltpu.make_async_copy(value, out, sems.at[4 + n]))
+    for copy in copies:
+        copy.start()
+    for copy in copies:
+        copy.wait()
+
+
+def stored(master, first, second, weights):
+    return pl.pallas_call(
+        store_kernel,
+        out_shape=tuple(jax.ShapeDtypeStruct(v.shape, v.dtype) for v in (master, first, second, weights)),
+        in_specs=[pl.BlockSpec(memory_space=pltpu.VMEM)] * 4,
+        out_specs=(pl.BlockSpec(memory_space=pltpu.HBM),) * 4,
+        scratch_shapes=[pltpu.SemaphoreType.DMA((7,))],
+        compiler_params=pltpu.CompilerParams(vmem_limit_bytes=2 * 1024 * 1024),
+    )(master, first, second, weights)
 
 
 def to_rows(array):
@@ -675,8 +708,8 @@
 
 
 def on_device(activations, out_grads, master, first_moment, second_moment):
-    new_master, new_first, new_second, weights = fused(
-        activations, out_grads, to_rows(master), to_rows(first_moment), to_rows(second_moment)
+    new_master, new_first, new_second, weights = stored(
+        *fused(activations, out_grads, to_rows(master), to_rows(first_moment), to_rows(second_moment))
     )
     return (
         from_rows(new_master),

time: 123 us -> 98.9 us (0.80)
  local copies, waits for them, and re-layouts: 14.8 us -> 0 us
  Pallas kernels: 107 us -> 98.1 us
    unnamed x4 -> x0, local copies, waits for them, and re-layouts: 14.8 us -> none
    pallas_call x1 -> x2, Pallas kernels: 107 us -> 98.1 us  [the longest x1 93.8 us: fused(): pl.pallas_call(kernel, out_shape=(vmem((rows, LANES), F32), vmem((rows, L...]
where the time goes in v2:
time: 98.9 us; the launch traced here: 98.7 us
  Pallas kernels  98.1 us (99%)
    pallas_call x1, Pallas kernels, fused(): pl.pallas_call(kernel, out_shape=(vmem((rows, LANES), F32), vmem((rows, L...  93.8 us
    pallas_call x1, Pallas kernels, stored(): pl.pallas_call(store_kernel, out_shape=tuple((jax.ShapeDtypeStruct(v.shap...  4.31 us

profile of v2, /device:TPU:1, one launch (start us, length us, event | category | flops | bytes accessed | tf_op | source)
XLA Modules:
  0.0 98.7 jit_solution(11007421516057922031)
XLA Ops:
  0.6 93.8 %shard_map.84 = (f32[2048,128]{1,0:T(8,128)S(1)}, f32[2048,128]{1,0:T(8,128)S(1)}, f32[2048,128]{1,0:T(8,128)S(1)}, bf16[16,2048,128]{2,1,0:T(8,128)(2,1)S(1)}) custom-call(bf16[2,1024,1024]{2,1,0:T(8,128)(2,1)} %acts_hbm.1, bf16[2,1024,2048]{2,1,0:T(8,128)(2,1)} %grads_hbm.1, f32[2048,128]{1,0:T(8,128)} %bitcast.35, f32[2048,128]{1,0:T(8,128)} %bitcast.36, ...), custom_call_target="tpu_custom_call" | custom-call | tf_op jit(solution)/shard_map/pallas_call | solution.py:659
  94.4 4.3 %shard_map.85 = (f32[2048,128]{1,0:T(8,128)}, f32[2048,128]{1,0:T(8,128)}, f32[2048,128]{1,0:T(8,128)}, bf16[16,2048,128]{2,1,0:T(8,128)(2,1)}) custom-call(f32[2048,128]{1,0:T(8,128)S(1)} %get-tuple-element.12.master, f32[2048,128]{1,0:T(8,128)S(1)} %get-tuple-element.13.first, f32[2048,128]{1,0:T(8,128)S(1)} %get-tuple-element.14.second, ...), custom_call_target="tpu_custom_call" | custom-call | tf_op jit(solution)/shard_map/pallas_call | solution.py:690

commit v3 on v2

v3 whole, which is shorter than its diff:
```python
import functools
import math

import jax
import jax.numpy as jnp
from jax import lax
from jax.experimental import pallas as pl
from jax.experimental.pallas import tpu as pltpu
from jax.sharding import Mesh
from jax.sharding import PartitionSpec as P

DP = ("dp_0", "dp_1", "dp_2")
TP_DP = ("tp_0", "tp_1", "dp_0", "dp_1", "dp_2")
TP = ("tp_0", "tp_1")
MESH = pl.DeviceIdType.MESH
F32 = jnp.float32
BF16 = jnp.bfloat16


beta_first = 0.9
beta_second = 0.95
first_fix = 1.0 - 0.9**10
second_fix = 1.0 - 0.95**10
learn_rate = 0.01
decay_rate = 0.1
epsilon = 1e-08
limit_scale = 2.0

OWN = 64
WIDE = 256
HALF = WIDE // 2
STEPS = 8
X_PIECES = STEPS - 1
Z_PIECES = STEPS + 1
LANES = 128
GATHERS = 4
X_ROWS = 288
Z_ROWS = 224
SUB = 32
LAG_TWO = 5
LAG_THREE = 8
LAG_END = 12
TOP = 2.0**120
TINY = 1e-37


def encode(value):
    square = value * value
    fourth = square * square
    return (fourth * (square * (value * jnp.abs(value)))).astype(BF16)


def decode(code):
    power = code.astype(F32)
    half = lax.rsqrt(jnp.maximum(jnp.abs(power), TINY))
    eighth = lax.rsqrt(lax.rsqrt(half))
    return (power * half) * (eighth * (eighth * eighth))


def kernel(
    acts_hbm, grads_hbm, master_hbm, first_hbm, second_hbm,
    master_out, first_out, second_out, weights_out,
    acts, turned, outs, master, first, second, own_grad,
    pair_send, pair_recv, total,
    x1_send, x1_recv, xz1_send, xz1_recv, xz2_send, xz2_recv,
    zz1_send, zz1_recv, zz2_send, zz2_recv, zx_send, zx_recv,
    bound, bounds, norm_dp, norm_tp, squares_ref,
    load_sem, out_sem, state_sem, pair_ssem, pair_rsem, x1_ssem, x1_rsem, xz1_ssem, xz1_rsem, xz2_ssem, xz2_rsem,
    zz1_ssem, zz1_rsem, zz2_ssem, zz2_rsem, zx_ssem, zx_rsem,
    bound_ssem, bound_rsem, ndp_ssem, ndp_rsem, ntp_ssem, ntp_rsem,
    gx_ssem, gx_rsem, gz_ssem, gz_rsem, gd_ssem, gd_rsem,
):
    ny, nh = lax.axis_size("tp_0"), lax.axis_size("tp_1")
    y, h = lax.axis_index("tp_0"), lax.axis_index("tp_1")
    z, x, c = lax.axis_index("dp_0"), lax.axis_index("dp_1"), lax.axis_index("dp_2")
    nt = ny * nh
    dp_me = z * 4 + x * 2 + c
    tp_me = y * nh + h
    za, zb, zo = lax.rem(z + 1, 4), lax.rem(z + 3, 4), lax.rem(z + 2, 4)
    xo = 1 - x
    tokens = acts_hbm.shape[1]
    to_core = {"dp_2": 1 - c}
    to_x = {"dp_1": xo}
    to_za = {"dp_0": za}
    to_zb = {"dp_0": zb}

    def dp_of(k):
        other = lax.rem(dp_me + k, 16)
        return other, {"dp_0": other // 4, "dp_1": lax.rem(other // 2, 2), "dp_2": lax.rem(other, 2)}

    def tp_of(k):
        other = lax.rem(tp_me + k, nt)
        return other, {"tp_0": other // nh, "tp_1": lax.rem(other, nh)}

    def remote(src, dst, ssem, rsem, device):
        return pltpu.make_async_remote_copy(
            src_ref=src, dst_ref=dst, send_sem=ssem, recv_sem=rsem, device_id=device, device_id_type=MESH
        )

    def arrived(ref, rsem):
        remote(ref, ref, gd_ssem, rsem, to_core).wait_recv()

    def left(ref, ssem):
        remote(ref, ref, ssem, gd_rsem, to_core).wait_send()

    def acts_load(l):
        return pltpu.make_async_copy(acts_hbm.at[l], acts.at[l], load_sem.at[l])

    def outs_load(i):
        return pltpu.make_async_copy(
            grads_hbm.at[i // 4, :, pl.ds(pl.multiple_of(lax.rem(i, 4) * (2 * WIDE), 2 * WIDE), 2 * WIDE)],
            outs.at[i],
            out_sem.at[i],
        )

    states = (
        pltpu.make_async_copy(master_hbm, master, state_sem.at[0]),
        pltpu.make_async_copy(first_hbm, first, state_sem.at[1]),
        pltpu.make_async_copy(second_hbm, second, state_sem.at[2]),
    )
    acts_load(0).start()
    outs_load(0).start()
    acts_load(1).start()

    def start_outs(i, carry):
        outs_load(i).start()
        return carry

    lax.fori_loop(1, STEPS, start_outs, 0)
    for copy in states:
        copy.start()

    barrier = pltpu.get_barrier_semaphore()

    def greet_dp(k, carry):
        pl.semaphore_signal(barrier, inc=1, device_id=dp_of(k)[1], device_id_type=MESH)
        return carry

    def greet_tp(k, carry):
        pl.semaphore_signal(barrier, inc=1, device_id=tp_of(k)[1], device_id_type=MESH)
        return carry

    lax.fori_loop(1, 16, greet_dp, 0)
    lax.fori_loop(1, nt, greet_tp, 0)

    def turn(l):
        for q in range(8):
            flipped = acts[l, :, q * LANES : (q + 1) * LANES].T
            turned[l, 0, q * OWN : (q + 1) * OWN, :] = flipped[:OWN]
            turned[l, 1, q * OWN : (q + 1) * OWN, :] = flipped[OWN:]

    def largest(ref, lead):
        rows, wide = ref.shape[1], ref.shape[2]

        def step(r, best):
            part = jnp.abs(ref[lead, pl.ds(pl.multiple_of(r * 64, 64), 64), :])
            return jnp.maximum(best, jnp.max(part.reshape(4, 16, wide), axis=0))

        return lax.fori_loop(0, rows // 64, step, jnp.zeros((16, wide), BF16))

    acts_load(0).wait()
    turn(0)

    def product(l, core, i, p):
        return jnp.dot(
            turned[l, core], outs[i, :, p * WIDE : (p + 1) * WIDE], preferred_element_type=F32
        ).reshape(8, OWN, WIDE)

    def pair_copy(i, p):
        slot = lax.rem(i, 2)
        return remote(pair_send.at[slot, p], pair_recv.at[i, p], pair_ssem.at[slot], pair_rsem.at[i, p], to_core)

    def multiply(i):
        l = i // 4
        slot = lax.rem(i, 2)

        @pl.when(i >= 2)
        def _():
            left(pair_send.at[slot], pair_ssem.at[slot])

        pair_send[slot, 0] = product(l, 1 - c, i, 0)
        pair_send[slot, 1] = product(l, 1 - c, i, 1)
        pair_copy(i, 0).start()
        total[i, 0] = product(l, c, i, 0)
        pair_copy(i, 1).start()
        total[i, 1] = product(l, c, i, 1)

    outs_load(0).wait()
    for p in range(2):
        pair_send[0, p] = product(0, 1 - c, 0, p)
        total[0, p] = product(0, c, 0, p)

    acts_load(1).wait()
    turn(1)
    biggest_act = jnp.maximum(jnp.max(largest(acts, 0).astype(F32)), jnp.max(largest(acts, 1).astype(F32)))
    best = largest(outs, 0)

    def widen(i, best):
        outs_load(i).wait()
        return jnp.maximum(best, largest(outs, i))

    best = lax.fori_loop(1, STEPS, widen, best)
    biggest_out = jnp.max(best.astype(F32))
    own_bound = jnp.maximum(biggest_act * biggest_out * (1.01 * tokens), 1e-30)
    bounds[dp_me] = jnp.full((8, LANES), own_bound, F32)
    bound[...] = jnp.full((8, LANES), own_bound, F32)
    mate = z * 4 + x * 2 + 1 - c

    pl.semaphore_wait(barrier, 15 + nt - 1)
    remote(bound, bounds.at[dp_me], bound_ssem, bound_rsem.at[0], to_core).start()
    for p in range(2):
        pair_copy(0, p).start()

    def bound_send(k, carry):
        other, device = dp_of(k)

        @pl.when(other != mate)
        def _():
            remote(bound, bounds.at[dp_me], bound_ssem, bound_rsem.at[1], device).start()

        return carry

    lax.fori_loop(1, 16, bound_send, 0)

    top = TOP**0.125

    def chip_scale():
        return top / (bounds[dp_me] + bounds[mate])[0:1, 0:1]

    def paired(i, p, q):
        return total[i, p, q] + pair_recv[i, p, q]

    def x1_copy(i):
        return remote(x1_send.at[i], x1_recv.at[i], x1_ssem, x1_rsem.at[i], to_x)

    def send_z(send, recv, ssem, rsem, n):
        remote(send.at[n, 0], recv.at[n, 0], ssem, rsem.at[n], to_za).start()
        remote(send.at[n, 1], recv.at[n, 1], ssem, rsem.at[n], to_zb).start()

    def zx_copy(n):
        return remote(zx_send.at[n], zx_recv.at[n], zx_ssem, zx_rsem.at[n], to_x)

    lo, hi = slice(0, HALF), slice(HALF, WIDE)

    def z_pieces(work, i):
        def one(k, carry):
            work(i + k, i, 1 - k)
            return carry

        lax.fori_loop(0, 1 + i // (STEPS - 1), one, 0)

    def x_one(i):
        scale = chip_scale()
        pair_copy(i, 0).wait_recv()
        for zz in range(4):
            x1_send[i, zz] = encode(paired(i, 0, zz * 2 + xo) * scale)
        x1_copy(i).start()

    def z_one(n, i, p):
        scale = chip_scale()
        pair_copy(i, p).wait_recv()
        for xx in range(2):
            far = encode(paired(i, p, zo * 2 + xx) * scale)
            zz1_send[n, 0, 0, xx] = far[:, lo]
            zz1_send[n, 1, 0, xx] = far[:, hi]
            q = za * 2 + xx
            zz1_send[n, 0, 1, xx] = encode((total[i, p, q, :, hi] + pair_recv[i, p, q, :, hi]) * scale)
            q = zb * 2 + xx
            zz1_send[n, 1, 1, xx] = encode((total[i, p, q, :, lo] + pair_recv[i, p, q, :, lo]) * scale)
        send_z(zz1_send, zz1_recv, zz1_ssem, zz1_rsem, n)

    def bound_of(zz, xx):
        return (bounds[zz * 4 + xx * 2] + bounds[zz * 4 + xx * 2 + 1])[0:1, 0:1]

    def scales():
        whole = jnp.sum(bounds[...], axis=0)[0:1, 0:1] * 1.01
        return top / whole, whole * (1.0 / top)

    def from_z():
        return bound_of(za, x) * (1.0 / top), bound_of(zb, x) * (1.0 / top)

    def x_two(i):
        scale, unscale = scales()
        from_x = bound_of(z, xo) * (1.0 / top)
        x1_copy(i).wait_recv()
        for zz in range(4):
            q = zz * 2 + x
            total[i, 0, q] = paired(i, 0, q) + decode(x1_recv[i, zz]) * from_x
        far = encode(total[i, 0, zo * 2 + x] * scale)
        xz1_send[i, 0, 0] = far[:, lo]
        xz1_send[i, 1, 0] = far[:, hi]
        xz1_send[i, 0, 1] = encode(total[i, 0, za * 2 + x, :, hi] * scale)
        xz1_send[i, 1, 1] = encode(total[i, 0, zb * 2 + x, :, lo] * scale)
        send_z(xz1_send, xz1_recv, xz1_ssem, xz1_rsem, i)

    def z_two(n, i, p):
        scale, unscale = scales()
        from_za, from_zb = from_z()
        arrived(zz1_recv.at[n], zz1_rsem.at[n])
        for xx in range(2):
            q = za * 2 + xx
            mine = total[i, p, q, :, lo] + pair_recv[i, p, q, :, lo]
            zz2_send[n, 0, xx] = encode((mine + decode(zz1_recv[n, 0, 0, xx]) * from_zb) * scale)
            q = zb * 2 + xx
            mine = total[i, p, q, :, hi] + pair_recv[i, p, q, :, hi]
            zz2_send[n, 1, xx] = encode((mine + decode(zz1_recv[n, 1, 0, xx]) * from_za) * scale)
        send_z(zz2_send, zz2_recv, zz2_ssem, zz2_rsem, n)

    def x_three(i):
        scale, unscale = scales()
        arrived(xz1_recv.at[i], xz1_rsem.at[i])
        xz2_send[i, 0] = encode(total[i, 0, za * 2 + x, :, lo] * scale + decode(xz1_recv[i, 0, 0]))
        xz2_send[i, 1] = encode(total[i, 0, zb * 2 + x, :, hi] * scale + decode(xz1_recv[i, 1, 0]))
        send_z(xz2_send, xz2_recv, xz2_ssem, xz2_rsem, i)

    def z_three(n, i, p):
        scale, unscale = scales()
        from_za, from_zb = from_z()
        arrived(zz2_recv.at[n], zz2_rsem.at[n])

        def summed(xx):
            q = z * 2 + xx
            low = (
                total[i, p, q, :, lo] + pair_recv[i, p, q, :, lo]
                + decode(zz1_recv[n, 1, 1, xx]) * from_za + decode(zz2_recv[n, 0, xx]) * unscale
            )
            high = (
                total[i, p, q, :, hi] + pair_recv[i, p, q, :, hi]
                + decode(zz1_recv[n, 0, 1, xx]) * from_zb + decode(zz2_recv[n, 1, xx]) * unscale
            )
            return low, high

        low, high = summed(xo)
        zx_send[n, :, lo] = encode(low * scale)
        zx_send[n, :, hi] = encode(high * scale)
        zx_copy(n).start()
        low, high = summed(x)
        total[i, p, z * 2 + x, :, lo] = low
        total[i, p, z * 2 + x, :, hi] = high

    def put(i, j, value):
        base = (lax.rem(i, 4) * 4 + j) * 2 + i // 4
        for r in range(OWN // 8):
            own_grad[pl.ds(base + r * 8 * 32, 8, stride=32), :] = value[r * 8 : (r + 1) * 8]
        return jnp.sum((value * value).reshape(OWN // 8, 8, LANES), axis=0)

    def x_end(i):
        unscale = scales()[1]
        arrived(xz2_recv.at[i], xz2_rsem.at[i])
        q = z * 2 + x
        g = total[i, 0, q, :, lo] + (decode(xz1_recv[i, 1, 1]) + decode(xz2_recv[i, 0])) * unscale
        squares = squares_ref[...] + put(i, 0, g)
        g = total[i, 0, q, :, hi] + (decode(xz1_recv[i, 0, 1]) + decode(xz2_recv[i, 1])) * unscale
        squares_ref[...] = squares + put(i, 1, g)

    def z_end(n, i, p):
        unscale = scales()[1]
        zx_copy(n).wait_recv()
        g = total[i, p, z * 2 + x] + decode(zx_recv[n]) * unscale
        squares = squares_ref[...] + put(i, 2 * p, g[:, lo])
        squares_ref[...] = squares + put(i, 2 * p + 1, g[:, hi])

    def turn_of(t, carry):
        def during(lag, count, work):
            @pl.when((t >= lag) & (t < lag + count))
            def _():
                work(t - lag)

        during(0, STEPS, multiply)

        @pl.when(t == 1)
        def _():
            arrived(bound, bound_rsem.at[0])

        during(1, X_PIECES, x_one)
        during(1, STEPS, functools.partial(z_pieces, z_one))

        @pl.when(t == LAG_TWO)
        def _():
            arrived(bounds.at[pl.ds(0, 14)], bound_rsem.at[1])

        during(LAG_TWO, X_PIECES, x_two)
        during(LAG_TWO, STEPS, functools.partial(z_pieces, z_two))
        during(LAG_THREE, X_PIECES, x_three)
        during(LAG_THREE, STEPS, functools.partial(z_pieces, z_three))
        during(LAG_END, X_PIECES, x_end)
        during(LAG_END, STEPS, functools.partial(z_pieces, z_end))
        return carry

    squares_ref[...] = jnp.zeros((8, LANES), F32)
    lax.fori_loop(1, LAG_END + STEPS, turn_of, 0)

    norm_dp[dp_me] = squares_ref[...]

    def ndp_send(k, carry):
        place = norm_dp.at[dp_me]
        remote(place, place, ndp_ssem, ndp_rsem, dp_of(k)[1]).start()
        return carry

    def ntp_send(k, carry):
        place = norm_tp.at[tp_me]
        remote(place, place, ntp_ssem, ntp_rsem, tp_of(k)[1]).start()
        return carry

    lax.fori_loop(1, 16, ndp_send, 0)
    arrived(norm_dp.at[pl.ds(0, 15)], ndp_rsem)
    norm_tp[tp_me] = jnp.sum(norm_dp[...], axis=0)
    lax.fori_loop(1, nt, ntp_send, 0)
    for copy in states:
        copy.wait()
    if nt > 1:
        arrived(norm_tp.at[pl.ds(0, nt - 1)], ntp_rsem)
    sum_squares = jnp.sum(jnp.sum(norm_tp[...], axis=0), keepdims=True)
    entries = OWN * 16 * nt * 2 * 2048
    limit = limit_scale * math.sqrt(entries)
    clip_factor = limit / jnp.maximum(jnp.sqrt(sum_squares), limit)

    def update(start):
        rows = pl.ds(pl.multiple_of(start, SUB), SUB)
        clipped = clip_factor * own_grad[rows, :]
        new_first = beta_first * first[rows, :] + (1.0 - beta_first) * clipped
        new_second = beta_second * second[rows, :] + (1.0 - beta_second) * clipped * clipped
        step_dir = new_first * (1.0 / first_fix) / (jnp.sqrt(new_second * (1.0 / second_fix)) + epsilon)
        old = master[rows, :]
        new_master = old - learn_rate * (step_dir + decay_rate * old)
        first_out[rows, :] = new_first
        second_out[rows, :] = new_second
        master_out[rows, :] = new_master
        weights_out[dp_me, rows, :] = new_master.astype(BF16)

    def x_part(k):
        return pl.ds(pl.multiple_of(k * X_ROWS, 16), X_ROWS)

    def z_part(k):
        return pl.ds(pl.multiple_of(GATHERS * X_ROWS + k * Z_ROWS, 16), Z_ROWS)

    def x_half(k, n):
        return pl.ds(pl.multiple_of(k * X_ROWS + n * (X_ROWS // 2), 16), X_ROWS // 2)

    def z_half(k, n):
        return pl.ds(pl.multiple_of(GATHERS * X_ROWS + k * Z_ROWS + n * (Z_ROWS // 2), 16), Z_ROWS // 2)

    def move(zz, xx, rows, ssem, rsem, device):
        place = weights_out.at[zz * 4 + xx * 2 + c, rows, :]
        return remote(place, place, ssem, rsem, device)

    def gx(k, n, zz, xx, rows):
        return move(zz, xx, rows, gx_ssem, gx_rsem.at[k, n], to_x)

    def gz(k, n, zz, xx, rows, device):
        return move(zz, xx, rows, gz_ssem, gz_rsem.at[k, n], device)

    def gd(zz, xx, rows):
        return move(zz, xx, rows, gd_ssem, gd_rsem, to_core)

    def z_cross(k, zz):
        gx(k, 1, zz, x, z_part(k)).start()

    def blocks(count, rows):
        return weights_out.at[pl.ds(0, count), pl.ds(0, rows), :]

    def spread(k, n, xx, rows):
        gz(k, n, z, xx, rows, to_za).start()
        gz(k, n, z, xx, rows, to_zb).start()

    def halves(k, n, xx, half):
        gz(k, n, zb, xx, half(k, 0), to_za).start()
        gz(k, n, za, xx, half(k, 1), to_zb).start()

    def update_loop(k, carry):
        def in_x(s, carry):
            update(k * X_ROWS + s * SUB)
            return carry

        def in_z(s, carry):
            update(GATHERS * X_ROWS + k * Z_ROWS + s * SUB)
            return carry

        lax.fori_loop(0, X_ROWS // SUB, in_x, 0)
        gx(k, 0, z, x, x_part(k)).start()
        gd(z, x, x_part(k)).start()
        lax.fori_loop(0, Z_ROWS // SUB, in_z, 0)
        spread(k, 3, x, z_part(k))
        gd(z, x, z_part(k)).start()
        return carry

    lax.fori_loop(0, GATHERS, update_loop, 0)

    def own_loop(k, carry):
        z_cross(k, z)
        spread(k, 0, x, x_part(k))
        return carry

    lax.fori_loop(0, GATHERS, own_loop, 0)

    def hop_one(k):
        arrived(blocks(1, X_ROWS), gx_rsem.at[k, 0])
        spread(k, 1, xo, x_part(k))
        gd(z, xo, x_part(k)).start()
        arrived(blocks(2, Z_ROWS), gz_rsem.at[k, 3])
        halves(k, 4, x, z_half)
        for zz in (zb, za):
            z_cross(k, zz)
            gd(zz, x, z_part(k)).start()

    def hop_two(k):
        for n, xx in ((0, x), (1, xo)):
            arrived(blocks(2, X_ROWS), gz_rsem.at[k, n])
            halves(k, 2, xx, x_half)
            for zz in (zb, za):
                gd(zz, xx, x_part(k)).start()
        arrived(blocks(1, Z_ROWS), gz_rsem.at[k, 4])
        z_cross(k, zo)
        gd(zo, x, z_part(k)).start()

    def hop_three(k):
        arrived(blocks(4, Z_ROWS), gx_rsem.at[k, 1])
        for zz in (z, zb, za, zo):
            gd(zz, xo, z_part(k)).start()
        arrived(blocks(2, X_ROWS), gz_rsem.at[k, 2])
        for xx in (x, xo):
            gd(zo, xx, x_part(k)).start()

    hop_one(0)
    hop_one(1)
    hop_two(0)

    def gather_loop(k, carry):
        hop_one(k)
        hop_two(k - 1)
        hop_three(k - 2)
        return carry

    lax.fori_loop(2, GATHERS, gather_loop, 0)
    hop_two(GATHERS - 1)
    hop_three(GATHERS - 2)
    hop_three(GATHERS - 1)

    for slot in range(2):
        left(pair_send.at[slot], pair_ssem.at[slot])
    for sent, ssem in (
        (x1_send, x1_ssem), (xz1_send, xz1_ssem), (xz2_send, xz2_ssem), (zz1_send, zz1_ssem), (zz2_send, zz2_ssem),
        (zx_send, zx_ssem), (bounds.at[pl.ds(0, 15)], bound_ssem), (norm_dp.at[pl.ds(0, 15)], ndp_ssem),
        (blocks(4, X_ROWS + 4 * Z_ROWS), gx_ssem), (blocks(8, GATHERS * (6 * X_ROWS + 3 * Z_ROWS) // 8), gz_ssem),
        (blocks(8, OWN * 32), gd_ssem),
    ):
        left(sent, ssem)
    if nt > 1:
        left(norm_tp.at[pl.ds(0, nt - 1)], ntp_ssem)
    arrived(blocks(8, OWN * 32), gd_rsem)


def fused(acts, grads, master, first, second):
    tokens = acts.shape[1]
    rows = OWN * 32
    dma = pltpu.SemaphoreType.DMA
    vmem = pltpu.VMEM
    scratch = [
        vmem((2, tokens, 1024), BF16),
        vmem((2, 2, 512, tokens), BF16),
        vmem((STEPS, tokens, 2 * WIDE), BF16),
        vmem((rows, LANES), F32),
        vmem((rows, LANES), F32),
        vmem((rows, LANES), F32),
        vmem((rows, LANES), F32),
        vmem((2, 2, 8, OWN, WIDE), F32),
        vmem((STEPS, 2, 8, OWN, WIDE), F32),
        vmem((STEPS, 2, 8, OWN, WIDE), F32),
    ]
    for shape in (
        (X_PIECES, 4, OWN, WIDE),
        (X_PIECES, 2, 2, OWN, HALF),
        (X_PIECES, 2, OWN, HALF),
        (Z_PIECES, 2, 2, 2, OWN, HALF),
        (Z_PIECES, 2, 2, OWN, HALF),
        (Z_PIECES, OWN, WIDE),
    ):
        scratch += [vmem(shape, BF16), vmem(shape, BF16)]
    tp = lax.axis_size("tp_0") * lax.axis_size("tp_1")
    scratch += [
        vmem((8, LANES), F32),
        vmem((16, 8, LANES), F32),
        vmem((16, 8, LANES), F32),
        vmem((tp, 8, LANES), F32),
        vmem((8, LANES), F32),
        dma((2,)), dma((STEPS,)), dma((3,)),
        dma((2,)), dma((STEPS, 2)),
        dma, dma((X_PIECES,)),
        dma, dma((X_PIECES,)),
        dma, dma((X_PIECES,)),
        dma, dma((Z_PIECES,)),
        dma, dma((Z_PIECES,)),
        dma, dma((Z_PIECES,)),
        dma, dma((2,)),
        dma, dma,
        dma, dma,
        dma, dma((GATHERS, 2)),
        dma, dma((GATHERS, 5)),
        dma, dma,
    ]
    anywhere = pl.BlockSpec(memory_space=pl.ANY)
    inside = pl.BlockSpec(memory_space=pltpu.VMEM)
    return pl.pallas_call(
        kernel,
        out_shape=(
            vmem((rows, LANES), F32),
            vmem((rows, LANES), F32),
            vmem((rows, LANES), F32),
            vmem((16, rows, LANES), BF16),
        ),
        in_specs=[anywhere] * 5,
        out_specs=(inside,) * 4,
        scratch_shapes=scratch,
        compiler_params=pltpu.CompilerParams(
            collective_id=0, has_side_effects=True, vmem_limit_bytes=50 * 1024 * 1024
        ),
    )(acts, grads, master, first, second)


def store_kernel(master, first, second, weights, master_out, first_out, second_out, weights_out, sems):
    copies = [
        pltpu.make_async_copy(weights.at[pl.ds(4 * n, 4)], weights_out.at[pl.ds(4 * n, 4)], sems.at[n])
        for n in range(4)
    ]
    for n, (value, out) in enumerate(((master, master_out), (first, first_out), (second, second_out))):
        copies.append(pltpu.make_async_copy(value, out, sems.at[4 + n]))
    for copy in copies:
        copy.start()
    for copy in copies:
        copy.wait()


def stored(master, first, second, weights):
    return pl.pallas_call(
        store_kernel,
        out_shape=tuple(jax.ShapeDtypeStruct(v.shape, v.dtype) for v in (master, first, second, weights)),
        in_specs=[pl.BlockSpec(memory_space=pltpu.VMEM)] * 4,
        out_specs=(pl.BlockSpec(memory_space=pltpu.HBM),) * 4,
        scratch_shapes=[pltpu.SemaphoreType.DMA((7,))],
        compiler_params=pltpu.CompilerParams(vmem_limit_bytes=2 * 1024 * 1024),
    )(master, first, second, weights)


def to_rows(array):
    own = array.shape[0]
    return array.reshape(own, 2, 16, LANES).swapaxes(1, 2).reshape(own * 32, LANES)


def from_rows(array):
    own = array.shape[0] // 32
    return array.reshape(own, 16, 2, LANES).swapaxes(1, 2).reshape(own, 2, 2048)


def on_device(activations, out_grads, master, first_moment, second_moment):
    new_master, new_first, new_second, weights = stored(
        *fused(activations, out_grads, to_rows(master), to_rows(first_moment), to_rows(second_moment))
    )
    return (
        from_rows(new_master),
        from_rows(new_first),
        from_rows(new_second),
        from_rows(weights.reshape(-1, LANES)),
    )


def solution(mesh):
    finer = Mesh(mesh.devices.reshape(4, 2, 4, 2, 2), ("tp_0", "tp_1", "dp_0", "dp_1", "dp_2"))
    in_specs = (
        P(None, DP, TP),
        P(None, DP, None),
        P(TP_DP, None, None),
        P(TP_DP, None, None),
        P(TP_DP, None, None),
    )
    out_specs = (
        P(TP_DP, None, None),
        P(TP_DP, None, None),
        P(TP_DP, None, None),
        P(TP, None, None),
    )
    return jax.shard_map(
        on_device, mesh=finer, in_specs=in_specs, out_specs=out_specs, check_vma=False
    )
```

time: 98.9 us -> 96.5 us (0.976)
  Pallas kernels: 98.1 us -> 95.8 us
    pallas_call x1, Pallas kernels: 93.8 us -> 91.5 us  [fused(): pl.pallas_call(kernel, out_shape=(vmem((rows, LANES), F32), vmem((rows, L...]
where the time goes in v3:
time: 96.5 us; the launch traced here: 96.4 us
  Pallas kernels  95.8 us (99%)
    pallas_call x1, Pallas kernels, fused(): pl.pallas_call(kernel, out_shape=(vmem((rows, LANES), F32), vmem((rows, L...  91.5 us
    pallas_call x1, Pallas kernels, stored(): pl.pallas_call(store_kernel, out_shape=tuple((jax.ShapeDtypeStruct(v.shap...  4.31 us

profile of v3, /device:TPU:1, one launch (start us, length us, event | category | flops | bytes accessed | tf_op | source)
XLA Modules:
  0.0 96.4 jit_solution(17659293617937292873)
XLA Ops:
  0.6 91.5 %shard_map.84 = (f32[2048,128]{1,0:T(8,128)S(1)}, f32[2048,128]{1,0:T(8,128)S(1)}, f32[2048,128]{1,0:T(8,128)S(1)}, bf16[16,2048,128]{2,1,0:T(8,128)(2,1)S(1)}) custom-call(bf16[2,1024,1024]{2,1,0:T(8,128)(2,1)} %acts_hbm.1, bf16[2,1024,2048]{2,1,0:T(8,128)(2,1)} %grads_hbm.1, f32[2048,128]{1,0:T(8,128)} %bitcast.35, f32[2048,128]{1,0:T(8,128)} %bitcast.36, ...), custom_call_target="tpu_custom_call" | custom-call | tf_op jit(solution)/shard_map/pallas_call | solution.py:603
  92.1 4.3 %shard_map.85 = (f32[2048,128]{1,0:T(8,128)}, f32[2048,128]{1,0:T(8,128)}, f32[2048,128]{1,0:T(8,128)}, bf16[16,2048,128]{2,1,0:T(8,128)(2,1)}) custom-call(f32[2048,128]{1,0:T(8,128)S(1)} %get-tuple-element.12.master, f32[2048,128]{1,0:T(8,128)S(1)} %get-tuple-element.13.first, f32[2048,128]{1,0:T(8,128)S(1)} %get-tuple-element.14.second, ...), custom_call_target="tpu_custom_call" | custom-call | tf_op jit(solution)/shard_map/pallas_call | solution.py:634

commit v4 on v3

--- a/solution.py
+++ b/solution.py
@@ -37,9 +37,9 @@
 X_ROWS = 288
 Z_ROWS = 224
 SUB = 32
-LAG_TWO = 5
-LAG_THREE = 8
-LAG_END = 12
+LAG_TWO = 3
+LAG_THREE = 6
+LAG_END = 9
 TOP = 2.0**120
 TINY = 1e-37
 
@@ -521,18 +521,20 @@
         for xx in (x, xo):
             gd(zo, xx, x_part(k)).start()
 
-    hop_one(0)
-    hop_one(1)
+    def first_hops(k, carry):
+        hop_one(k)
+        return carry
+
+    lax.fori_loop(0, GATHERS, first_hops, 0)
     hop_two(0)
+    hop_two(1)
 
     def gather_loop(k, carry):
-        hop_one(k)
-        hop_two(k - 1)
+        hop_two(k)
         hop_three(k - 2)
         return carry
 
     lax.fori_loop(2, GATHERS, gather_loop, 0)
-    hop_two(GATHERS - 1)
     hop_three(GATHERS - 2)
     hop_three(GATHERS - 1)
 
@@ -541,7 +543,7 @@
     for sent, ssem in (
         (x1_send, x1_ssem), (xz1_send, xz1_ssem), (xz2_send, xz2_ssem), (zz1_send, zz1_ssem), (zz2_send, zz2_ssem),
         (zx_send, zx_ssem), (bounds.at[pl.ds(0, 15)], bound_ssem), (norm_dp.at[pl.ds(0, 15)], ndp_ssem),
-        (blocks(4, X_ROWS + 4 * Z_ROWS), gx_ssem), (blocks(8, GATHERS * (6 * X_ROWS + 3 * Z_ROWS) // 8), gz_ssem),
+        (blocks(8, GATHERS * (X_ROWS + 4 * Z_ROWS) // 8), gx_ssem), (blocks(8, GATHERS * (6 * X_ROWS + 3 * Z_ROWS) // 8), gz_ssem),
         (blocks(8, OWN * 32), gd_ssem),
     ):
         left(sent, ssem)

time: 96.5 us -> 93.5 us (0.969)
  Pallas kernels: 95.8 us -> 92.7 us
    pallas_call x1, Pallas kernels: 91.5 us -> 88.4 us  [fused(): pl.pallas_call(kernel, out_shape=(vmem((rows, LANES), F32), vmem((rows, L...]
where the time goes in v4:
time: 93.5 us; the launch traced here: 93.4 us
  Pallas kernels  92.7 us (99%)
    pallas_call x1, Pallas kernels, fused(): pl.pallas_call(kernel, out_shape=(vmem((rows, LANES), F32), vmem((rows, L...  88.4 us
    pallas_call x1, Pallas kernels, stored(): pl.pallas_call(store_kernel, out_shape=tuple((jax.ShapeDtypeStruct(v.shap...  4.31 us

profile of v4, /device:TPU:1, one launch (start us, length us, event | category | flops | bytes accessed | tf_op | source)
XLA Modules:
  0.0 93.4 jit_solution(6960997107158647831)
XLA Ops:
  0.6 88.4 %shard_map.84 = (f32[2048,128]{1,0:T(8,128)S(1)}, f32[2048,128]{1,0:T(8,128)S(1)}, f32[2048,128]{1,0:T(8,128)S(1)}, bf16[16,2048,128]{2,1,0:T(8,128)(2,1)S(1)}) custom-call(bf16[2,1024,1024]{2,1,0:T(8,128)(2,1)} %acts_hbm.1, bf16[2,1024,2048]{2,1,0:T(8,128)(2,1)} %grads_hbm.1, f32[2048,128]{1,0:T(8,128)} %bitcast.35, f32[2048,128]{1,0:T(8,128)} %bitcast.36, ...), custom_call_target="tpu_custom_call" | custom-call | tf_op jit(solution)/shard_map/pallas_call | solution.py:605
  89.1 4.3 %shard_map.85 = (f32[2048,128]{1,0:T(8,128)}, f32[2048,128]{1,0:T(8,128)}, f32[2048,128]{1,0:T(8,128)}, bf16[16,2048,128]{2,1,0:T(8,128)(2,1)}) custom-call(f32[2048,128]{1,0:T(8,128)S(1)} %get-tuple-element.12.master, f32[2048,128]{1,0:T(8,128)S(1)} %get-tuple-element.13.first, f32[2048,128]{1,0:T(8,128)S(1)} %get-tuple-element.14.second, ...), custom_call_target="tpu_custom_call" | custom-call | tf_op jit(solution)/shard_map/pallas_call | solution.py:636

commit v5 on v4

--- a/solution.py
+++ b/solution.py
@@ -36,7 +36,8 @@
 GATHERS = 4
 X_ROWS = 288
 Z_ROWS = 224
-SUB = 32
+X_SUB = 96
+Z_SUB = 112
 LAG_TWO = 3
 LAG_THREE = 6
 LAG_END = 9
@@ -379,12 +380,12 @@
         def _():
             arrived(bounds.at[pl.ds(0, 14)], bound_rsem.at[1])
 
+        during(LAG_TWO, STEPS, functools.partial(z_pieces, z_two))
+        during(LAG_THREE, STEPS, functools.partial(z_pieces, z_three))
+        during(LAG_END, STEPS, functools.partial(z_pieces, z_end))
         during(LAG_TWO, X_PIECES, x_two)
-        during(LAG_TWO, STEPS, functools.partial(z_pieces, z_two))
         during(LAG_THREE, X_PIECES, x_three)
-        during(LAG_THREE, STEPS, functools.partial(z_pieces, z_three))
         during(LAG_END, X_PIECES, x_end)
-        during(LAG_END, STEPS, functools.partial(z_pieces, z_end))
         return carry
 
     squares_ref[...] = jnp.zeros((8, LANES), F32)
@@ -415,8 +416,8 @@
     limit = limit_scale * math.sqrt(entries)
     clip_factor = limit / jnp.maximum(jnp.sqrt(sum_squares), limit)
 
-    def update(start):
-        rows = pl.ds(pl.multiple_of(start, SUB), SUB)
+    def update(start, count):
+        rows = pl.ds(pl.multiple_of(start, 16), count)
         clipped = clip_factor * own_grad[rows, :]
         new_first = beta_first * first[rows, :] + (1.0 - beta_first) * clipped
         new_second = beta_second * second[rows, :] + (1.0 - beta_second) * clipped * clipped
@@ -469,17 +470,17 @@
 
     def update_loop(k, carry):
         def in_x(s, carry):
-            update(k * X_ROWS + s * SUB)
+            update(k * X_ROWS + s * X_SUB, X_SUB)
             return carry
 
         def in_z(s, carry):
-            update(GATHERS * X_ROWS + k * Z_ROWS + s * SUB)
+            update(GATHERS * X_ROWS + k * Z_ROWS + s * Z_SUB, Z_SUB)
             return carry
 
-        lax.fori_loop(0, X_ROWS // SUB, in_x, 0)
+        lax.fori_loop(0, X_ROWS // X_SUB, in_x, 0)
         gx(k, 0, z, x, x_part(k)).start()
         gd(z, x, x_part(k)).start()
-        lax.fori_loop(0, Z_ROWS // SUB, in_z, 0)
+        lax.fori_loop(0, Z_ROWS // Z_SUB, in_z, 0)
         spread(k, 3, x, z_part(k))
         gd(z, x, z_part(k)).start()
         return carry

time: 93.5 us -> 93.3 us (level)
  no operation moved by 1% of the time
where the time goes in v5:
time: 93.3 us; the launch traced here: 93.1 us
  Pallas kernels  92.5 us (99%)
    pallas_call x1, Pallas kernels, fused(): pl.pallas_call(kernel, out_shape=(vmem((rows, LANES), F32), vmem((rows, L...  88.2 us
    pallas_call x1, Pallas kernels, stored(): pl.pallas_call(store_kernel, out_shape=tuple((jax.ShapeDtypeStruct(v.shap...  4.31 us

profile of v5, /device:TPU:1, one launch (start us, length us, event | category | flops | bytes accessed | tf_op | source)
XLA Modules:
  0.0 93.1 jit_solution(16384983580163645651)
XLA Ops:
  0.6 88.2 %shard_map.84 = (f32[2048,128]{1,0:T(8,128)S(1)}, f32[2048,128]{1,0:T(8,128)S(1)}, f32[2048,128]{1,0:T(8,128)S(1)}, bf16[16,2048,128]{2,1,0:T(8,128)(2,1)S(1)}) custom-call(bf16[2,1024,1024]{2,1,0:T(8,128)(2,1)} %acts_hbm.1, bf16[2,1024,2048]{2,1,0:T(8,128)(2,1)} %grads_hbm.1, f32[2048,128]{1,0:T(8,128)} %bitcast.35, f32[2048,128]{1,0:T(8,128)} %bitcast.36, ...), custom_call_target="tpu_custom_call" | custom-call | tf_op jit(solution)/shard_map/pallas_call | solution.py:606
  88.8 4.3 %shard_map.85 = (f32[2048,128]{1,0:T(8,128)}, f32[2048,128]{1,0:T(8,128)}, f32[2048,128]{1,0:T(8,128)}, bf16[16,2048,128]{2,1,0:T(8,128)(2,1)}) custom-call(f32[2048,128]{1,0:T(8,128)S(1)} %get-tuple-element.12.master, f32[2048,128]{1,0:T(8,128)S(1)} %get-tuple-element.13.first, f32[2048,128]{1,0:T(8,128)S(1)} %get-tuple-element.14.second, ...), custom_call_target="tpu_custom_call" | custom-call | tf_op jit(solution)/shard_map/pallas_call | solution.py:637

commit v6 on v5

--- a/solution.py
+++ b/solution.py
@@ -33,9 +33,9 @@
 X_PIECES = STEPS - 1
 Z_PIECES = STEPS + 1
 LANES = 128
-GATHERS = 4
-X_ROWS = 288
-Z_ROWS = 224
+GATHERS = 2
+X_ROWS = 576
+Z_ROWS = 448
 X_SUB = 96
 Z_SUB = 112
 LAG_TWO = 3
@@ -403,10 +403,12 @@
         remote(place, place, ntp_ssem, ntp_rsem, tp_of(k)[1]).start()
         return carry
 
-    lax.fori_loop(1, 16, ndp_send, 0)
+    for k in range(1, 16):
+        ndp_send(k, 0)
     arrived(norm_dp.at[pl.ds(0, 15)], ndp_rsem)
     norm_tp[tp_me] = jnp.sum(norm_dp[...], axis=0)
-    lax.fori_loop(1, nt, ntp_send, 0)
+    for k in range(1, nt):
+        ntp_send(k, 0)
     for copy in states:
         copy.wait()
     if nt > 1:
@@ -454,19 +456,15 @@
     def gd(zz, xx, rows):
         return move(zz, xx, rows, gd_ssem, gd_rsem, to_core)
 
-    def z_cross(k, zz):
-        gx(k, 1, zz, x, z_part(k)).start()
+    def z_cross(k, n, zz):
+        gx(k, n, zz, x, z_part(k)).start()
 
     def blocks(count, rows):
         return weights_out.at[pl.ds(0, count), pl.ds(0, rows), :]
 
     def spread(k, n, xx, rows):
         gz(k, n, z, xx, rows, to_za).start()
-        gz(k, n, z, xx, rows, to_zb).start()
-
-    def halves(k, n, xx, half):
-        gz(k, n, zb, xx, half(k, 0), to_za).start()
-        gz(k, n, za, xx, half(k, 1), to_zb).start()
+        gz(k, n + 1, z, xx, rows, to_zb).start()
 
     def update_loop(k, carry):
         def in_x(s, carry):
@@ -481,14 +479,14 @@
         gx(k, 0, z, x, x_part(k)).start()
         gd(z, x, x_part(k)).start()
         lax.fori_loop(0, Z_ROWS // Z_SUB, in_z, 0)
-        spread(k, 3, x, z_part(k))
+        spread(k, 4, x, z_part(k))
         gd(z, x, z_part(k)).start()
         return carry
 
     lax.fori_loop(0, GATHERS, update_loop, 0)
 
     def own_loop(k, carry):
-        z_cross(k, z)
+        z_cross(k, 1, z)
         spread(k, 0, x, x_part(k))
         return carry
 
@@ -496,30 +494,35 @@
 
     def hop_one(k):
         arrived(blocks(1, X_ROWS), gx_rsem.at[k, 0])
-        spread(k, 1, xo, x_part(k))
+        spread(k, 2, xo, x_part(k))
         gd(z, xo, x_part(k)).start()
-        arrived(blocks(2, Z_ROWS), gz_rsem.at[k, 3])
-        halves(k, 4, x, z_half)
-        for zz in (zb, za):
-            z_cross(k, zz)
-            gd(zz, x, z_part(k)).start()
+        arrived(blocks(1, Z_ROWS), gz_rsem.at[k, 4])
+        gz(k, 8, zb, x, z_half(k, 0), to_za).start()
+        z_cross(k, 2, zb)
+        gd(zb, x, z_part(k)).start()
+        arrived(blocks(1, Z_ROWS), gz_rsem.at[k, 5])
+        gz(k, 8, za, x, z_half(k, 1), to_zb).start()
+        z_cross(k, 3, za)
+        gd(za, x, z_part(k)).start()
 
     def hop_two(k):
         for n, xx in ((0, x), (1, xo)):
-            arrived(blocks(2, X_ROWS), gz_rsem.at[k, n])
-            halves(k, 2, xx, x_half)
-            for zz in (zb, za):
-                gd(zz, xx, x_part(k)).start()
-        arrived(blocks(1, Z_ROWS), gz_rsem.at[k, 4])
-        z_cross(k, zo)
+            arrived(blocks(1, X_ROWS), gz_rsem.at[k, 2 * n])
+            gz(k, 6 + n, zb, xx, x_half(k, 0), to_za).start()
+            gd(zb, xx, x_part(k)).start()
+            arrived(blocks(1, X_ROWS), gz_rsem.at[k, 2 * n + 1])
+            gz(k, 6 + n, za, xx, x_half(k, 1), to_zb).start()
+            gd(za, xx, x_part(k)).start()
+        arrived(blocks(1, Z_ROWS), gz_rsem.at[k, 8])
+        z_cross(k, 4, zo)
         gd(zo, x, z_part(k)).start()
 
     def hop_three(k):
-        arrived(blocks(4, Z_ROWS), gx_rsem.at[k, 1])
-        for zz in (z, zb, za, zo):
+        for n, zz in ((1, z), (2, zb), (3, za), (4, zo)):
+            arrived(blocks(1, Z_ROWS), gx_rsem.at[k, n])
             gd(zz, xo, z_part(k)).start()
-        arrived(blocks(2, X_ROWS), gz_rsem.at[k, 2])
-        for xx in (x, xo):
+        for n, xx in ((6, x), (7, xo)):
+            arrived(blocks(1, X_ROWS), gz_rsem.at[k, n])
             gd(zo, xx, x_part(k)).start()
 
     def first_hops(k, carry):
@@ -597,8 +600,8 @@
         dma, dma((2,)),
         dma, dma,
         dma, dma,
-        dma, dma((GATHERS, 2)),
         dma, dma((GATHERS, 5)),
+        dma, dma((GATHERS, 9)),
         dma, dma,
     ]
     anywhere = pl.BlockSpec(memory_space=pl.ANY)

time: 93.3 us -> 93.1 us (level)
  no operation moved by 1% of the time
where the time goes in v6:
time: 93.1 us; the launch traced here: 93 us
  Pallas kernels  92.3 us (99%)
    pallas_call x1, Pallas kernels, fused(): pl.pallas_call(kernel, out_shape=(vmem((rows, LANES), F32), vmem((rows, L...  88 us
    pallas_call x1, Pallas kernels, stored(): pl.pallas_call(store_kernel, out_shape=tuple((jax.ShapeDtypeStruct(v.shap...  4.31 us

profile of v6, /device:TPU:1, one launch (start us, length us, event | category | flops | bytes accessed | tf_op | source)
XLA Modules:
  0.0 93.0 jit_solution(10673541582114687312)
XLA Ops:
  0.6 88.0 %shard_map.84 = (f32[2048,128]{1,0:T(8,128)S(1)}, f32[2048,128]{1,0:T(8,128)S(1)}, f32[2048,128]{1,0:T(8,128)S(1)}, bf16[16,2048,128]{2,1,0:T(8,128)(2,1)S(1)}) custom-call(bf16[2,1024,1024]{2,1,0:T(8,128)(2,1)} %acts_hbm.1, bf16[2,1024,2048]{2,1,0:T(8,128)(2,1)} %grads_hbm.1, f32[2048,128]{1,0:T(8,128)} %bitcast.35, f32[2048,128]{1,0:T(8,128)} %bitcast.36, ...), custom_call_target="tpu_custom_call" | custom-call | tf_op jit(solution)/shard_map/pallas_call | solution.py:609
  88.7 4.3 %shard_map.85 = (f32[2048,128]{1,0:T(8,128)}, f32[2048,128]{1,0:T(8,128)}, f32[2048,128]{1,0:T(8,128)}, bf16[16,2048,128]{2,1,0:T(8,128)(2,1)}) custom-call(f32[2048,128]{1,0:T(8,128)S(1)} %get-tuple-element.12.master, f32[2048,128]{1,0:T(8,128)S(1)} %get-tuple-element.13.first, f32[2048,128]{1,0:T(8,128)S(1)} %get-tuple-element.14.second, ...), custom_call_target="tpu_custom_call" | custom-call | tf_op jit(solution)/shard_map/pallas_call | solution.py:640

commit v7 on v6

--- a/solution.py
+++ b/solution.py
@@ -39,8 +39,8 @@
 X_SUB = 96
 Z_SUB = 112
 LAG_TWO = 3
-LAG_THREE = 6
-LAG_END = 9
+LAG_THREE = 5
+LAG_END = 8
 TOP = 2.0**120
 TINY = 1e-37
 

time: 93.1 us -> 93.3 us (level)
  no operation moved by 1% of the time
where the time goes in v7:
time: 93.3 us; the launch traced here: 93.2 us
  Pallas kernels  92.5 us (99%)
    pallas_call x1, Pallas kernels, fused(): pl.pallas_call(kernel, out_shape=(vmem((rows, LANES), F32), vmem((rows, L...  88.2 us
    pallas_call x1, Pallas kernels, stored(): pl.pallas_call(store_kernel, out_shape=tuple((jax.ShapeDtypeStruct(v.shap...  4.31 us

profile of v7, /device:TPU:1, one launch (start us, length us, event | category | flops | bytes accessed | tf_op | source)
XLA Modules:
  0.0 93.2 jit_solution(5359576771535815957)
XLA Ops:
  0.6 88.2 %shard_map.84 = (f32[2048,128]{1,0:T(8,128)S(1)}, f32[2048,128]{1,0:T(8,128)S(1)}, f32[2048,128]{1,0:T(8,128)S(1)}, bf16[16,2048,128]{2,1,0:T(8,128)(2,1)S(1)}) custom-call(bf16[2,1024,1024]{2,1,0:T(8,128)(2,1)} %acts_hbm.1, bf16[2,1024,2048]{2,1,0:T(8,128)(2,1)} %grads_hbm.1, f32[2048,128]{1,0:T(8,128)} %bitcast.35, f32[2048,128]{1,0:T(8,128)} %bitcast.36, ...), custom_call_target="tpu_custom_call" | custom-call | tf_op jit(solution)/shard_map/pallas_call | solution.py:609
  88.9 4.3 %shard_map.85 = (f32[2048,128]{1,0:T(8,128)}, f32[2048,128]{1,0:T(8,128)}, f32[2048,128]{1,0:T(8,128)}, bf16[16,2048,128]{2,1,0:T(8,128)(2,1)}) custom-call(f32[2048,128]{1,0:T(8,128)S(1)} %get-tuple-element.12.master, f32[2048,128]{1,0:T(8,128)S(1)} %get-tuple-element.13.first, f32[2048,128]{1,0:T(8,128)S(1)} %get-tuple-element.14.second, ...), custom_call_target="tpu_custom_call" | custom-call | tf_op jit(solution)/shard_map/pallas_call | solution.py:640
